TPU v7x, 256 devices: a whole 4x4x8 slice. The times are simulated.
256 devices in a mesh: dp: 32 (over x, y, z_hi), mp: 8 (over z_lo, core).
Axes of the slice: x: 4, y: 4, z: 8 (z_hi: 2, z_lo: 4; z = z_hi * 4 + z_lo), core: 2. Of those that a mesh axis runs over, the one named last changes fastest.
Arguments:
- tokens: bfloat16 [1024, 7168], P('dp', 'mp'), may hold values from -6 to 6
- gate_weight: bfloat16 [7168, 18432], P('mp', 'dp'), may hold values from -0.0625 to 0.0625
- up_weight: bfloat16 [7168, 18432], P('mp', 'dp'), may hold values from -0.0625 to 0.0625
- down_weight: bfloat16 [18432, 7168], P('dp', 'mp'), may hold values from -0.046875 to 0.046875
- gate_round: bfloat16 [7168, 18432], P('mp', 'dp'), may hold values from -8 to 8
- up_round: bfloat16 [7168, 18432], P('mp', 'dp'), may hold values from -8 to 8
- down_round: bfloat16 [18432, 7168], P('dp', 'mp'), may hold values from -8 to 8
- quant_scale: float32 [2, 18432], P(None, 'dp'), may hold values from 0.3 to 3
- quant_bits: int32 [2, 18432], P(None, 'dp'), may hold values from 2 to 4
- quant_zero: int32 [2, 18432], P(None, 'dp'), may hold values from 0 to 2
- down_scale: float32 [7168], P('mp'), may hold values from 0.3 to 3
- down_bits: int32 [7168], P('mp'), may hold values from 2 to 4
- down_zero: int32 [7168], P('mp'), may hold values from 0 to 2
- fisher: float32 [1024], replicated, may hold values from 1 to 300, as said below
Outputs:
- loss_value: float32 [], replicated
- grad_gate: bfloat16 [7168, 18432], P('mp', 'dp')
- grad_up: bfloat16 [7168, 18432], P('mp', 'dp')
- grad_down: bfloat16 [18432, 7168], P('dp', 'mp')
Inputs may be any that keep to these rules, and one draw needn't show every extreme that they name: `fisher`: positive weights.
All inputs are finite; a program needn't handle non-finite values.
Results may differ from a plain program's by a relative error of at most 0.0059.
Values may be sent and summed in bfloat16 or wider, within the bound.
No kernel may reach another device: no remote copies, remote signals or barrier semaphores. Data moves between devices by JAX's collectives and lax.ppermute only.
A program may use at most 128 MiB of HBM per device.

v0:
```python
import jax
import jax.numpy as jnp
from jax import lax
from jax.sharding import Mesh
from jax.sharding import PartitionSpec as P

D = 7168
FF = 18432
DP = ("dp_0", "dp_1", "dp_2")
MP = ("mp_0", "mp_1")
DP_MP = ("dp_0", "dp_1", "dp_2", "mp_0", "mp_1")


def in_order(tiles, dim):
    tiles = jnp.moveaxis(tiles, 0, dim)
    shape = tiles.shape
    return tiles.reshape(*shape[:dim], shape[dim] * shape[dim + 1], *shape[dim + 2 :])


def copy_for_each(value, axis):
    copies = jnp.broadcast_to(value, (lax.axis_size(axis), *value.shape))
    return lax.all_to_all(copies, axis, split_axis=0, concat_axis=0, tiled=True)


def gathered_copies(value, axis, dim):
    return in_order(copy_for_each(value, axis), dim)


def scatter_axes(value, axes, dim):
    if not axes:
        return value
    nearer = lax.psum_scatter(value, axes[0], scatter_dimension=dim, tiled=True)
    return scatter_axes(nearer, axes[1:], dim)


def over_axes(value, axes):
    for axis in axes:
        value = lax.psum(value, axis)
    return value


def split_up(value, dim, count):
    shape = value.shape
    tiles = value.reshape(*shape[:dim], count, shape[dim] // count, *shape[dim + 1 :])
    return jnp.moveaxis(tiles, dim, 0)


def sent_and_summed(value, axis, dim):
    count = lax.axis_size(axis)
    tiles = lax.all_to_all(split_up(value, dim, count), axis, 0, 0, tiled=True)
    return jnp.sum(tiles, axis=0)


def soft_weight(weight, variable, channel_scale, bit_width, zero_point, fan_in):
    quant_step = channel_scale / jnp.sqrt(jnp.float32(fan_in))
    offset = jnp.clip(1.2 * jax.nn.sigmoid(variable.astype(jnp.float32)) - 0.1, 0.0, 1.0)
    ceiling = (jnp.left_shift(jnp.int32(1), bit_width) - 1).astype(jnp.float32)
    zero_level = zero_point.astype(jnp.float32)
    levels = jnp.clip(
        weight.astype(jnp.float32) / quant_step + offset - 0.5 + zero_level, 0.0, ceiling
    )
    return (quant_step * (levels - zero_level)).astype(jnp.bfloat16)


def contract_rows(left, right):
    return lax.dot_general(
        left, right, (((0,), (0,)), ((), ())), preferred_element_type=jnp.float32
    )


def shards(
    tokens,
    gate_weight,
    up_weight,
    down_weight,
    gate_round,
    up_round,
    down_round,
    quant_scale,
    quant_bits,
    quant_zero,
    down_scale,
    down_bits,
    down_zero,
    fisher,
):
    own_rows = tokens.shape[0]
    hidden_cols = gate_weight.shape[1]
    all_tokens = lax.all_gather(tokens, DP, axis=0, tiled=True)
    total_rows = all_tokens.shape[0]
    gate_student = soft_weight(
        gate_weight, gate_round, quant_scale[0], quant_bits[0], quant_zero[0], D
    )
    up_student = soft_weight(up_weight, up_round, quant_scale[1], quant_bits[1], quant_zero[1], D)
    stacked = jnp.concatenate([gate_weight, up_weight, gate_student, up_student], axis=1)
    partial_value = jnp.dot(all_tokens, stacked, preferred_element_type=jnp.float32)
    shares = lax.psum_scatter(partial_value, MP, scatter_dimension=0, tiled=True)
    gate_teacher = shares[:, :hidden_cols]
    up_teacher = shares[:, hidden_cols : 2 * hidden_cols]
    gate_own = shares[:, 2 * hidden_cols : 3 * hidden_cols]
    up_own = shares[:, 3 * hidden_cols :]
    hidden_teacher = (jax.nn.silu(gate_teacher) * up_teacher).astype(jnp.bfloat16)
    hidden_student = (jax.nn.silu(gate_own) * up_own).astype(jnp.bfloat16)
    hidden = gathered_copies(jnp.concatenate([hidden_teacher, hidden_student], axis=1), MP, 0)
    down_student = soft_weight(down_weight, down_round, down_scale, down_bits, down_zero, FF)
    terms = jnp.dot(
        hidden,
        jnp.concatenate([-down_weight, down_student], axis=0),
        preferred_element_type=jnp.float32,
    )
    summed = scatter_axes(terms, DP, 0)
    token_weight = lax.dynamic_slice_in_dim(fisher, lax.axis_index(DP) * own_rows, own_rows)
    weighted = token_weight[:, None] * summed
    partial_loss = jnp.sum(weighted * summed)
    local_grad = (2.0 * weighted).astype(jnp.bfloat16)
    loss_sum = over_axes(partial_loss, DP_MP)
    out_grad = lax.all_gather(local_grad, DP, axis=0, tiled=True)
    loss_value = loss_sum / (total_rows * D)
    grad_down = contract_rows(hidden[:, hidden_cols:], out_grad).astype(jnp.bfloat16)
    hidden_part = lax.dot_general(
        out_grad, down_student, (((1,), (1,)), ((), ())), preferred_element_type=jnp.float32
    )
    hidden_grad = sent_and_summed(hidden_part, MP, 0)
    sigmoid_gate = jax.nn.sigmoid(gate_own)
    gate_grad = (
        hidden_grad * up_own * sigmoid_gate * (1.0 + gate_own * (1.0 - sigmoid_gate))
    ).astype(jnp.bfloat16)
    up_grad = (hidden_grad * gate_own * sigmoid_gate).astype(jnp.bfloat16)
    both_grads = gathered_copies(jnp.concatenate([gate_grad, up_grad], axis=1), MP, 0)
    weight_grads = contract_rows(all_tokens, both_grads)
    grad_gate = weight_grads[:, :hidden_cols].astype(jnp.bfloat16)
    grad_up = weight_grads[:, hidden_cols:].astype(jnp.bfloat16)
    return (loss_value, grad_gate, grad_up, grad_down)


def solution(mesh):
    split = Mesh(mesh.devices.reshape(4, 4, 2, 4, 2), ("dp_0", "dp_1", "dp_2", "mp_0", "mp_1"))
    return jax.shard_map(
        shards,
        mesh=split,
        in_specs=(
            P(DP, MP),
            P(MP, DP),
            P(MP, DP),
            P(DP, MP),
            P(MP, DP),
            P(MP, DP),
            P(DP, MP),
            P(None, DP),
            P(None, DP),
            P(None, DP),
            P(MP),
            P(MP),
            P(MP),
            P(),
        ),
        out_specs=(P(), P(MP, DP), P(MP, DP), P(DP, MP)),
        check_vma=False,
    )
```

profile of v0, /device:TPU:65, one launch (start us, length us, event | category | flops | bytes accessed | tf_op | source)
XLA Modules:
  0.0 616.8 jit_solution(13538513241438266588)
XLA Ops:
  7.2 0.0 all-gather.3.cloned.1.call-start
  7.2 0.7 all-gather.3.cloned.1.call-update
  7.9 0.0 reduce-scatter.5.cloned.1.call-start
  7.9 0.8 convert_reduce_fusion.2
  8.7 0.8 multiply_reduce_fusion.1
  9.5 0.8 convert_reduce_fusion.3
  10.3 4.8 multiply_convert_fusion.1
  15.1 83.8 %all-gather.3.cloned.1.call-done = bf16[1024,896]{1,0:T(8,128)(2,1)} async-done(((bf16[32,896]{1,0:T(8,128)(2,1)}), bf16[1024,896]{1,0:T(8,128)(2,1)}) %all-gather.3.cloned.1.call-update) | async-done | bytes 1835024 | tf_op jit(solution)/shard_map/all_gather | solution.py:89
  99.0 11.9 %convolution_bitcast_fusion = f32[1024,2304]{0,1:T(8,128)} fusion(bf16[1024,896]{1,0:T(8,128)(2,1)} %all-gather.3.cloned.1.call-done, bf16[896,576]{0,1:T(8,128)(2,1)S(1)} %get-tuple-element.18, bf16[896,576]{0,1:T(8,128)(2,1)} %get-tuple-element.19, bf16[896,576]{0,1:T(8,128)(2,1)S(1)} %copy-done.6, bf16[896,576]{0,1:T(8,128)(2,1)S(1)} %copy-done.7), kind=kOutput, calls=%fused_computation | convolution fusion | flops 4244373504 | bytes 15400960 | tf_op jit(solution)/shard_map/dot_general | solution.py:96
  110.9 0.0 reduce-scatter.5.cloned.1.call-update
  110.9 100.8 %reduce-scatter.5.cloned.1.call-done = f32[128,2304]{0,1:T(8,128)} async-done(((f32[1024,2304]{0,1:T(8,128)}), f32[128,2304]{0,1:T(8,128)}) %reduce-scatter.5.cloned.1.call-update) | async-done | bytes 1179664 | tf_op jit(solution)/shard_map/reduce_scatter | solution.py:97
  211.7 1.4 fusion.13
  213.1 0.2 copy.20
  213.3 1.7 broadcast_in_dim.8
  215.1 6.0 all-to-all-start
  221.0 0.0 reduce-scatter.7.cloned.1.call-start
  221.1 1.1 neg.24
  222.3 0.2 copy-done.4
  222.5 2.1 multiply_convert_fusion
  224.7 47.2 %all-to-all-done = bf16[8,128,1152]{2,1,0:T(8,128)(2,1)S(1)} async-done(((bf16[8,128,1152]{2,1,0:T(8,128)(2,1)}), bf16[8,128,1152]{2,1,0:T(8,128)(2,1)S(1)}, u32[]{:S(2)}, u32[]{:S(2)}) %all-to-all-start) | async-done | bytes 2359328 | tf_op jit(solution)/shard_map/all_to_all | solution.py:22
  271.9 7.0 %fusion.8 = f32[1024,896]{1,0:T(8,128)} fusion(bf16[1024,1152]{1,0:T(8,128)(2,1)S(1)} %bitcast.19, bf16[576,896]{1,0:T(8,128)(2,1)} %multiply_convert_fusion, bf16[576,896]{1,0:T(8,128)(2,1)} %neg.24), kind=kOutput, calls=%fused_computation.11 | convolution fusion | flops 2118057984 | bytes 8093696 | tf_op jit(solution)/shard_map/dot_general | solution.py:106
  278.9 0.0 reduce-scatter.7.cloned.1.call-update
  278.9 0.0 reduce-scatter.9.cloned.1.call-start
  279.0 47.4 %reduce-scatter.7.cloned.1.call-done = f32[256,896]{1,0:T(8,128)} async-done(((f32[1024,896]{1,0:T(8,128)}), f32[256,896]{1,0:T(8,128)}) %reduce-scatter.7.cloned.1.call-update) | async-done | bytes 917520 | tf_op jit(solution)/shard_map/reduce_scatter | solution.py:32
  326.4 0.0 reduce-scatter.11.cloned.1.call-start
  326.4 26.6 %reduce-scatter.9.cloned.1.call-done = f32[64,896]{1,0:T(8,128)} async-done(((f32[256,896]{1,0:T(8,128)}), f32[64,896]{1,0:T(8,128)}) %reduce-scatter.9.cloned.1.call-update) | async-done | bytes 229392 | tf_op jit(solution)/shard_map/reduce_scatter | solution.py:32
  353.1 0.0 all-gather.5.cloned.1.call-start
  353.1 0.8 dynamic_slice.3
  353.9 23.4 %reduce-scatter.11.cloned.1.call-done = f32[32,896]{1,0:T(8,128)} async-done(((f32[64,896]{1,0:T(8,128)}), f32[32,896]{1,0:T(8,128)}) %reduce-scatter.11.cloned.1.call-update) | async-done | bytes 114704 | tf_op jit(solution)/shard_map/reduce_scatter | solution.py:32
  377.2 2.2 fusion.15
  379.5 85.6 %all-gather.5.cloned.1.call-done = bf16[1024,896]{1,0:T(8,128)(2,1)} async-done(((bf16[32,896]{1,0:T(8,128)(2,1)}), bf16[1024,896]{1,0:T(8,128)(2,1)}) %all-gather.5.cloned.1.call-update) | async-done | bytes 1835024 | tf_op jit(solution)/shard_map/all_gather | solution.py:117
  465.0 2.9 convolution_bitcast_fusion.1
  468.0 0.2 copy.25
  468.1 57.4 %all_to_all.15 = f32[8,128,576]{1,2,0:T(8,128)S(1)} all-to-all(f32[8,128,576]{1,2,0:T(8,128)S(1)} %bitcast.18), channel_id=1, replica_groups=mesh['dp_0'=4,'dp_1'=4,'dp_2'=2,'mp_0'=4,'mp_1'=2] {'mp_0','mp_1'}, dimensions={0} | all-to-all | bytes 4718592 | tf_op jit(solution)/shard_map/all_to_all | solution.py:50
  525.6 0.8 reduce_sum.19
  526.4 0.5 copy-done.1
  526.9 1.1 multiply_convert_fusion.4
  528.1 0.2 copy.22
  528.3 1.7 broadcast_in_dim.9
  530.0 8.4 %all-to-all-start.2 = ((bf16[8,128,1152]{2,1,0:T(8,128)(2,1)}), bf16[8,128,1152]{2,1,0:T(8,128)(2,1)}, u32[]{:S(2)}, u32[]{:S(2)}) async-start(bf16[8,128,1152]{2,1,0:T(8,128)(2,1)} %broadcast_in_dim.9), calls=%async_computation.6 | async-start | bytes 4718592 | tf_op jit(solution)/shard_map/all_to_all | solution.py:22
  538.4 7.8 %psum.35 = f32[]{:T(128)} all-reduce(f32[]{:T(128)} %get-tuple-element.17), channel_id=1, replica_groups=mesh['dp_0'=4,'dp_1'=4,'dp_2'=2,'mp_0'=4,'mp_1'=2] {'dp_0'}, use_global_device_ids=true, to_apply=%region_5.6 | all-reduce | flops 1 | bytes 8 | tf_op jit(solution)/shard_map/psum | solution.py:38
  546.2 8.5 %psum.36 = f32[]{:T(128)} all-reduce(f32[]{:T(128)} %psum.35), channel_id=1, replica_groups=mesh['dp_0'=4,'dp_1'=4,'dp_2'=2,'mp_0'=4,'mp_1'=2] {'dp_1'}, use_global_device_ids=true, to_apply=%region_6.7 | all-reduce | flops 1 | bytes 8 | tf_op jit(solution)/shard_map/psum | solution.py:38
  554.7 14.7 %psum.37 = f32[]{:T(128)} all-reduce(f32[]{:T(128)} %psum.36), channel_id=1, replica_groups=mesh['dp_0'=4,'dp_1'=4,'dp_2'=2,'mp_0'=4,'mp_1'=2] {'dp_2'}, use_global_device_ids=true, to_apply=%region_7.8 | all-reduce | flops 1 | bytes 8 | tf_op jit(solution)/shard_map/psum | solution.py:38
  569.4 23.5 %psum.38 = f32[]{:T(128)} all-reduce(f32[]{:T(128)} %psum.37), channel_id=1, replica_groups=mesh['dp_0'=4,'dp_1'=4,'dp_2'=2,'mp_0'=4,'mp_1'=2] {'mp_0'}, use_global_device_ids=true, to_apply=%region_8.9 | all-reduce | flops 1 | bytes 8 | tf_op jit(solution)/shard_map/psum | solution.py:38
  592.9 4.9 psum.39
  598.5 4.0 convolution_convert_fusion.1
  602.5 4.9 fusion.7
  607.4 1.5 fusion.18
  (29 shorter events, 0.2 us)
Async XLA Ops:
  7.2 91.8 %all-gather.3.cloned.1.call-start = ((), (), s32[]{:S(2)}) async-start(), calls=%async_computation.7 | async-start | bytes 1892352 | tf_op jit(solution)/shard_map/all_gather | solution.py:89
  7.9 203.8 %reduce-scatter.5.cloned.1.call-start = ((), (), s32[]{:S(2)}) async-start(), calls=%async_computation.8 | async-start | bytes 10616832 | tf_op jit(solution)/shard_map/reduce_scatter | solution.py:97
  10.3 88.7 %copy-start.6 = (bf16[896,576]{0,1:T(8,128)(2,1)S(1)}, bf16[896,576]{0,1:T(8,128)(2,1)}, u32[]{:S(2)}) copy-start(bf16[896,576]{0,1:T(8,128)(2,1)} %param.16) | copy-start | bytes 3096580
  10.3 88.6 %copy-start.7 = (bf16[896,576]{0,1:T(8,128)(2,1)S(1)}, bf16[896,576]{0,1:T(8,128)(2,1)}, u32[]{:S(2)}) copy-start(bf16[896,576]{0,1:T(8,128)(2,1)} %param.15) | copy-start | bytes 3096580
  215.1 6.0 copy-start.8
  215.1 6.1 copy-start
  215.1 56.8 %all-to-all-start = ((bf16[8,128,1152]{2,1,0:T(8,128)(2,1)}), bf16[8,128,1152]{2,1,0:T(8,128)(2,1)S(1)}, u32[]{:S(2)}, u32[]{:S(2)}) async-start(bf16[8,128,1152]{2,1,0:T(8,128)(2,1)} %broadcast_in_dim.8), calls=%async_computation.1 | async-start | bytes 4718592 | tf_op jit(solution)/shard_map/all_to_all | solution.py:22
  221.0 1.2 copy-start.9
  221.0 1.2 copy-start.10
  221.0 105.3 %reduce-scatter.7.cloned.1.call-start = ((), (), s32[]{:S(2)}) async-start(), calls=%async_computation.9 | async-start | bytes 4587520 | tf_op jit(solution)/shard_map/reduce_scatter | solution.py:32
  221.1 1.4 copy-start.4
  271.9 7.0 %copy-start.2 = (bf16[8,128,1152]{2,1,0:T(8,128)(2,1)}, bf16[8,128,1152]{2,1,0:T(8,128)(2,1)S(1)}, u32[]{:S(2)}) copy-start(bf16[8,128,1152]{2,1,0:T(8,128)(2,1)S(1)} %all-to-all-done) | copy-start | bytes 7077892
  278.9 186.2 %copy-start.5 = (bf16[576,896]{1,0:T(8,128)(2,1)S(1)}, bf16[576,896]{1,0:T(8,128)(2,1)}, u32[]{:S(2)}) copy-start(bf16[576,896]{1,0:T(8,128)(2,1)} %multiply_convert_fusion) | copy-start | bytes 3096580
  278.9 74.1 %reduce-scatter.9.cloned.1.call-start = ((), (), s32[]{:S(2)}) async-start(), calls=%async_computation.10 | async-start | bytes 1146880 | tf_op jit(solution)/shard_map/reduce_scatter | solution.py:32
  326.4 50.8 %reduce-scatter.11.cloned.1.call-start = ((), (), s32[]{:S(2)}) async-start(), calls=%async_computation.11 | async-start | bytes 344064 | tf_op jit(solution)/shard_map/reduce_scatter | solution.py:32
  353.1 112.0 %all-gather.5.cloned.1.call-start = ((), (), s32[]{:S(2)}) async-start(), calls=%async_computation.12 | async-start | bytes 1892352 | tf_op jit(solution)/shard_map/all_gather | solution.py:117
  525.6 1.4 copy-start.1
  530.0 68.5 %copy-start.3 = (bf16[8,128,1152]{2,1,0:T(8,128)(2,1)S(1)}, bf16[8,128,1152]{2,1,0:T(8,128)(2,1)}, u32[]{:S(2)}) copy-start(bf16[8,128,1152]{2,1,0:T(8,128)(2,1)} %copy-done.2) | copy-start | bytes 7077892
  530.0 72.5 %all-to-all-start.2 = ((bf16[8,128,1152]{2,1,0:T(8,128)(2,1)}), bf16[8,128,1152]{2,1,0:T(8,128)(2,1)}, u32[]{:S(2)}, u32[]{:S(2)}) async-start(bf16[8,128,1152]{2,1,0:T(8,128)(2,1)} %broadcast_in_dim.9), calls=%async_computation.6 | async-start | bytes 4718592 | tf_op jit(solution)/shard_map/all_to_all | solution.py:22
Sparse Core Ops, SparseCore 0:
  11.4 87.5 all-gather.2
  111.0 100.6 reduce-scatter.4
  279.0 47.2 reduce-scatter.6
  328.8 24.2 reduce-scatter.8
  355.4 21.8 reduce-scatter.10
  381.1 83.9 all-gather.4
where the time goes:
time: 618 us; the launch traced here: 617 us
  waiting for transfers between devices  415 us (67%)
  blocking collectives  117 us (19%)
  matrix products  30.7 us (5%)
  other arithmetic  16 us (3%)
  between operations  16 us (3%)
  starting transfers between devices  14.6 us (2%)
  local copies, waits for them, and re-layouts  7.04 us (1%)
    reduce_scatter x1, waiting for transfers between devices, shards(): lax.psum_scatter(partial_value, MP, scatter_dimension=0, tiled=True)  101 us
    reduce_scatter x3, waiting for transfers between devices, scatter_axes(): nearer = lax.psum_scatter(value, axes[0], scatter_dimension=dim, tiled=True)  97.4 us
    all_gather x1, waiting for transfers between devices, shards(): out_grad = lax.all_gather(local_grad, DP, axis=0, tiled=True)  85.6 us
    all_gather x1, waiting for transfers between devices, shards(): all_tokens = lax.all_gather(tokens, DP, axis=0, tiled=True)  83.8 us
    psum x5, blocking collectives, over_axes(): value = lax.psum(value, axis)  59.4 us
    all_to_all x1, blocking collectives, sent_and_summed(): tiles = lax.all_to_all(split_up(value, dim, count), axis, 0, 0, tiled=True)  57.4 us
    all_to_all x2, waiting for transfers between devices, copy_for_each(): return lax.all_to_all(copies, axis, split_axis=0, concat_axis=0, tiled=True)  47.2 us
    all_to_all x2, starting transfers between devices, copy_for_each(): return lax.all_to_all(copies, axis, split_axis=0, concat_axis=0, tiled=True)  14.4 us
  transfers between devices with their start and end apart: 8, of which 7 were waited for; matrix products, arithmetic and copies ran while one was open for 2% of the time, Pallas kernels for 0%

commit v1 on v0

v1 whole, which is shorter than its diff:
```python
import jax
import jax.numpy as jnp
import numpy as np
from jax import lax
from jax.sharding import Mesh
from jax.sharding import PartitionSpec as P


D = 7168
FF = 18432
X, Y, H, Z, C = "x", "y", "h", "z", "c"
SIZE = {X: 4, Y: 4, H: 2, Z: 4, C: 2}
SLOTS = (0, 2, 1, 3)
DP = (X, Y, H)
MP = (Z, C)
BF = jnp.bfloat16
F32 = jnp.float32


def product(left, right, left_dim, right_dim):
    return lax.dot_general(
        left, right, (((left_dim,), (right_dim,)), ((), ())), preferred_element_type=F32
    )


def flipped(value, axis, bit):
    return lax.ppermute(value, axis, [(i, i ^ bit) for i in range(SIZE[axis])])


def plane_groups():
    place = np.arange(256).reshape(4, 4, 2, 4, 2)
    return [
        [
            int(place[slot ^ z, 2 * (half ^ c) + low, h, z, c])
            for half in range(2)
            for slot in SLOTS
            for low in range(2)
        ]
        for h in range(2)
        for z in range(4)
        for c in range(2)
    ]


def exchange(blocks):
    return lax.all_to_all(
        blocks, (X, Y, H, Z, C), 0, 0, axis_index_groups=plane_groups(), tiled=True
    )


def copied(block):
    return jnp.broadcast_to(block, (16, *block.shape))


def gather_plane(block):
    return exchange(copied(block)).reshape(-1, block.shape[-1])


def scatter_plane(terms):
    blocks = terms.astype(BF).reshape(16, -1, terms.shape[-1])
    return jnp.sum(exchange(blocks).astype(F32), axis=0)


def halves_swapped(value):
    rows = value.shape[0] // 2
    return jnp.concatenate([value[rows:], value[:rows]], axis=0)


def slot_order(per_row):
    z, c = lax.axis_index(Z), lax.axis_index(C)
    table = per_row.reshape(2, 2, 2, 2, 2, -1)
    table = jnp.where(z & 1 == 1, table[:, ::-1], table)
    table = jnp.where(z & 2 == 2, table[::-1], table)
    table = jnp.where(c == 1, table[:, :, ::-1], table)
    table = jnp.where(lax.axis_index(H) == 1, table[:, :, :, :, ::-1], table)
    return table.transpose(2, 1, 0, 3, 4, 5).reshape(-1)


def together(value, *others):
    return lax.optimization_barrier((value, *others))


def joined(first, second):
    return jnp.concatenate([first, second], axis=0)


def added(value, axis, bit):
    return value + flipped(value, axis, bit)


def gathered_half(own):
    pair = joined(own, flipped(own, Z, 2))
    return joined(pair, flipped(pair, Z, 1))


def merged(first, second):
    shape = (-1, 32, first.shape[-1])
    both = jnp.stack([first.reshape(shape), second.reshape(shape)], axis=1)
    return both.reshape(-1, first.shape[-1])


def beside(first, second):
    return jnp.concatenate([first, second], axis=1)


def soft_weight(weight, variable, channel_scale, bit_width, zero_point, fan_in):
    quant_step = channel_scale / jnp.sqrt(jnp.float32(fan_in))
    offset = jnp.clip(1.2 * jax.nn.sigmoid(variable.astype(jnp.float32)) - 0.1, 0.0, 1.0)
    ceiling = (jnp.left_shift(jnp.int32(1), bit_width) - 1).astype(jnp.float32)
    zero_level = zero_point.astype(jnp.float32)
    levels = jnp.clip(
        weight.astype(jnp.float32) / quant_step + offset - 0.5 + zero_level, 0.0, ceiling
    )
    return (quant_step * (levels - zero_level)).astype(jnp.bfloat16)


def shards(
    tokens,
    gate_weight,
    up_weight,
    down_weight,
    gate_round,
    up_round,
    down_round,
    quant_scale,
    quant_bits,
    quant_zero,
    down_scale,
    down_bits,
    down_zero,
    fisher,
):
    hidden = gate_weight.shape[1]
    total_rows = fisher.shape[0]
    own_rows = tokens.shape[0]

    copies = copied(tokens)
    partner = flipped(tokens, H, 1)
    spread = exchange(copies)
    planes = [spread.reshape(-1, tokens.shape[-1]), None]
    (
        partner,
        copies,
        gate_weight,
        up_weight,
        gate_round,
        up_round,
        quant_scale,
        quant_bits,
        quant_zero,
    ) = together(
        partner,
        copies,
        gate_weight,
        up_weight,
        gate_round,
        up_round,
        quant_scale,
        quant_bits,
        quant_zero,
    )
    copies = copied(partner)
    spread = exchange(copies)
    planes[1] = spread.reshape(-1, tokens.shape[-1])

    gate_student = soft_weight(
        gate_weight, gate_round, quant_scale[0], quant_bits[0], quant_zero[0], D
    )
    up_student = soft_weight(up_weight, up_round, quant_scale[1], quant_bits[1], quant_zero[1], D)
    gates, ups = together(
        joined(gate_weight.T, gate_student.T), joined(up_weight.T, up_student.T)
    )
    row_weight = lax.dynamic_slice_in_dim(fisher, lax.axis_index((X, Y)) * 2 * own_rows, 2 * own_rows)
    row_weight = jnp.where(lax.axis_index(H) == 1, halves_swapped(row_weight), row_weight)
    slot_weight = slot_order(fisher)

    shares = []
    near_planes = []
    for k in range(2):
        half = planes[k].shape[0] // 2
        rows = half // 4
        full = [product(planes[k], weight, 1, 1) for weight in (gates, ups)]
        other = flipped(jnp.stack([part[half:].astype(BF) for part in full]), C, 1)
        own = jnp.stack([part[:half] for part in full]) + other
        given = own[:, 2 * rows :].astype(BF)
        if k == 0:
            planes[1], _ = together(planes[1], given)
        kept = own[:, : 2 * rows] + flipped(given, Z, 1)
        share = kept[:, :rows] + flipped(kept[:, rows:].astype(BF), Z, 2)
        shares.append(share)
        both = (jax.nn.silu(share[0]) * share[1]).astype(BF)
        near_planes.append(gathered_half(both))
    near = merged(*near_planes)
    far = flipped(near, C, 1)

    down_weight, down_round, _ = together(down_weight, down_round, shares[0])
    down_student = soft_weight(down_weight, down_round, down_scale, down_bits, down_zero, FF)
    downs, down_student = together(joined(-down_weight, down_student), down_student)

    all_tokens = merged(*planes)
    gate_own = merged(shares[0][0], shares[1][0])[:, hidden:]
    up_own = merged(shares[0][1], shares[1][1])[:, hidden:]
    sig = jax.nn.sigmoid(gate_own)
    factors = joined(
        (up_own * sig * (1.0 + gate_own * (1.0 - sig))).astype(BF).T,
        (gate_own * sig).astype(BF).T,
    )
    factors, _ = together(factors, far)

    terms = joined(
        product(near, downs, 1, 0).astype(BF), product(far, downs, 1, 0).astype(BF)
    )
    partial, received, all_tokens = together(
        scatter_plane(terms).astype(BF), flipped(factors, Z, 2), all_tokens
    )
    pair = beside(factors, received)
    residual = partial.astype(F32) + halves_swapped(flipped(partial, H, 1)).astype(F32)
    pair_grad = (2.0 * (row_weight[:, None] * residual)).astype(BF)
    out_grad, received = together(gather_plane(pair_grad), flipped(pair, Z, 1))
    near_factors = beside(pair, received)

    half = total_rows // 2
    rows = half // 4
    full = product(down_student, out_grad, 1, 1)
    other = flipped(full[:, half:].astype(BF), C, 1)
    given = (full[:, 2 * rows : half] + other[:, 2 * rows :]).astype(BF)
    kept = full[:, : 2 * rows] + other[:, : 2 * rows]
    wide, _ = together(out_grad, given)
    wide = wide.astype(F32)
    loss = jnp.full((8, 128), jnp.sum(wide * wide * (0.25 / slot_weight)[:, None]), F32)
    received, loss, far_factors = together(
        flipped(given, Z, 1), added(loss, C, 1), flipped(near_factors, C, 1)
    )
    kept = kept + received
    received, loss, near_down = together(
        flipped(kept[:, rows:].astype(BF), Z, 2),
        added(loss, Z, 1),
        product(near[:, hidden:], out_grad[:half], 0, 0),
    )
    own = (kept[:, :rows] + received).astype(BF)
    received, loss, grad_down = together(
        flipped(own, Z, 2),
        added(loss, Z, 2),
        (near_down + product(far[:, hidden:], out_grad[half:], 0, 0)).astype(BF),
    )
    pair = beside(own, received)
    near_grad = beside(pair, flipped(pair, Z, 1))
    far_grad = flipped(near_grad, C, 1)

    def weight_grad(first):
        def part(grad, factor, rows):
            scaled = grad.astype(F32) * factor[first : first + hidden]
            return product(scaled.astype(BF), rows, 1, 0)

        return part(near_grad, near_factors, all_tokens[:half]), lambda: part(
            far_grad, far_factors, all_tokens[half:]
        )

    gate_part, gate_rest = weight_grad(0)
    up_part, up_rest = weight_grad(hidden)
    far_grad, gate_part, up_part = together(far_grad, gate_part, up_part)
    grad_gate = (gate_part + gate_rest()).astype(BF)
    grad_up = (up_part + up_rest()).astype(BF)
    loss_value = loss[0, 0] / (total_rows * D)
    return (loss_value, grad_gate.T, grad_up.T, grad_down)


def solution(mesh):
    split = Mesh(mesh.devices.reshape(4, 4, 2, 4, 2), (X, Y, H, Z, C))
    return jax.shard_map(
        shards,
        mesh=split,
        in_specs=(
            P(DP, MP),
            P(MP, DP),
            P(MP, DP),
            P(DP, MP),
            P(MP, DP),
            P(MP, DP),
            P(DP, MP),
            P(None, DP),
            P(None, DP),
            P(None, DP),
            P(MP),
            P(MP),
            P(MP),
            P(),
        ),
        out_specs=(P(), P(MP, DP), P(MP, DP), P(DP, MP)),
        check_vma=False,
    )
```

time: 618 us -> 271 us (0.44)
  waiting for transfers between devices: 415 us -> 120 us
  blocking collectives: 117 us -> 0 us
  starting transfers between devices: 14.6 us -> 67.5 us
  other arithmetic: 16 us -> 32.5 us
  between operations: 16 us -> 3.12 us
  local copies, waits for them, and re-layouts: 7.04 us -> 17.9 us
    reduce_scatter x4 -> x0, waiting for transfers between devices: 198 us -> none  [the longest x1 101 us: shards(): lax.psum_scatter(partial_value, MP, scatter_dimension=0, tiled=True)]
    all_gather x2 -> x0, waiting for transfers between devices: 169 us -> none  [the longest x1 85.6 us: shards(): out_grad = lax.all_gather(local_grad, DP, axis=0, tiled=True)]
    ppermute x0 -> x25, waiting for transfers between devices: none -> 86.5 us  [flipped(): return lax.ppermute(value, axis, [(i, i ^ bit) for i in range(SIZE[axis])])]
    psum x5 -> x0, blocking collectives: 59.4 us -> none  [over_axes(): value = lax.psum(value, axis)]
    all_to_all x1 -> x0, blocking collectives: 57.4 us -> none  [sent_and_summed(): tiles = lax.all_to_all(split_up(value, dim, count), axis, 0, 0, tiled=True)]
    ppermute x0 -> x25, starting transfers between devices: none -> 33.3 us  [flipped(): return lax.ppermute(value, axis, [(i, i ^ bit) for i in range(SIZE[axis])])]
    all_to_all x2 -> x4, starting transfers between devices: 14.4 us -> 34.1 us  [exchange(): lax.all_to_all(blocks, (X, Y, H, Z, C), 0, 0, axis_index_groups=plane_gro...]
    all_to_all x2 -> x4, waiting for transfers between devices: 47.2 us -> 33.9 us  [exchange(): lax.all_to_all(blocks, (X, Y, H, Z, C), 0, 0, axis_index_groups=plane_gro...]
  transfers between devices with their start and end apart: 8 -> 29, of which waited for: 7 -> 18; matrix products, arithmetic and copies ran while one was open for 2% -> 19% of each run, Pallas kernels for 0% -> 0%
where the time goes in v1:
time: 271 us; the launch traced here: 266 us
  waiting for transfers between devices  120 us (44%)
  starting transfers between devices  67.5 us (25%)
  other arithmetic  32.5 us (12%)
  matrix products  24.8 us (9%)
  local copies, waits for them, and re-layouts  17.9 us (7%)
  between operations  3.12 us (1%)
    ppermute x25, waiting for transfers between devices, flipped(): return lax.ppermute(value, axis, [(i, i ^ bit) for i in range(SIZE[axis])])  86.5 us
    all_to_all x4, starting transfers between devices, exchange(): lax.all_to_all(blocks, (X, Y, H, Z, C), 0, 0, axis_index_groups=plane_gro...  34.1 us
    all_to_all x4, waiting for transfers between devices, exchange(): lax.all_to_all(blocks, (X, Y, H, Z, C), 0, 0, axis_index_groups=plane_gro...  33.9 us
    ppermute x25, starting transfers between devices, flipped(): return lax.ppermute(value, axis, [(i, i ^ bit) for i in range(SIZE[axis])])  33.3 us
    dot_general x13, matrix products, product(): lax.dot_general(left, right, (((left_dim,), (right_dim,)), ((), ())), pre...  24.8 us
  transfers between devices with their start and end apart: 29, of which 18 were waited for; matrix products, arithmetic and copies ran while one was open for 19% of the time, Pallas kernels for 0%

profile of v1, /device:TPU:65, one launch (start us, length us, event | category | flops | bytes accessed | tf_op | source)
XLA Modules:
  0.0 266.3 jit_solution(6179811932381708777)
XLA Ops:
  0.7 5.2 %collective-permute-start = (bf16[32,896]{1,0:T(8,128)(2,1)}, bf16[32,896]{1,0:T(8,128)(2,1)S(1)}, u32[]{:S(2)}, u32[]{:S(2)}) collective-permute-start(bf16[32,896]{1,0:T(8,128)(2,1)} %param.14), channel_id=1, source_target_pairs={{0,8},{8,0},{1,9},{9,1},{2,10},{10,2},{3,11},{11,3},{4,12},{12,4},... | collective-permute-start | bytes 172040 | tf_op jit(solution)/shard_map/ppermute | solution.py:27
  5.9 1.8 broadcast_in_dim.12
  7.7 8.9 %all-to-all-start = ((bf16[16,32,896]{2,1,0:T(8,128)(2,1)}), bf16[16,32,896]{2,1,0:T(8,128)(2,1)S(1)}, u32[]{:S(2)}, u32[]{:S(2)}) async-start(bf16[16,32,896]{2,1,0:T(8,128)(2,1)} %broadcast_in_dim.12), calls=%async_computation | async-start | bytes 1835008 | tf_op jit(solution)/shard_map/all_to_all | solution.py:46
  16.7 3.9 %fusion.6 = (bf16[576,896]{1,0:T(8,128)(2,1)S(1)}, bf16[576,896]{1,0:T(8,128)(2,1)S(1)}) fusion(f32[576]{0:T(1024)S(1)} %get-tuple-element.77, bf16[896,576]{0,1:T(8,128)(2,1)} %param.18, bf16[896,576]{0,1:T(8,128)(2,1)S(1)} %copy-done.2, f32[576]{0:T(1024)S(1)} %get-tuple-element.75, f32[576]{0:T(1024)S(1)} %get-tuple-element.73, ...), kind=kLoop, calls=%fused_computation.44 | loop fusion | flops 17547264 | bytes 6206976 | tf_op jit(solution)/shard_map/transpose | solution.py:171
  20.6 1.5 pad_maximum_fusion
  22.1 1.5 pad_maximum_fusion.1
  23.6 5.7 %all-to-all-done = bf16[16,32,896]{2,1,0:T(8,128)(2,1)S(1)} async-done(((bf16[16,32,896]{2,1,0:T(8,128)(2,1)}), bf16[16,32,896]{2,1,0:T(8,128)(2,1)S(1)}, u32[]{:S(2)}, u32[]{:S(2)}) %all-to-all-start) | async-done | bytes 917536 | tf_op jit(solution)/shard_map/all_to_all | solution.py:46
  29.3 3.5 %convolution_bitcast_fusion = f32[512,1152]{1,0:T(8,128)S(1)} fusion(bf16[1152,896]{1,0:T(8,128)(2,1)} %pad_maximum_fusion.1, bf16[512,896]{1,0:T(8,128)(2,1)S(1)} %bitcast.123), kind=kOutput, calls=%fused_computation.1 | convolution fusion | flops 1056964608 | bytes 5341184 | tf_op jit(solution)/shard_map/dot_general | solution.py:21
  32.9 1.5 convolution_bitcast_fusion.1
  37.6 6.8 %all-to-all-start.1 = ((bf16[16,32,896]{2,1,0:T(8,128)(2,1)}), bf16[16,32,896]{2,1,0:T(8,128)(2,1)S(1)}, u32[]{:S(2)}, u32[]{:S(2)}) async-start(bf16[16,32,896]{2,1,0:T(8,128)(2,1)} %broadcast_in_dim.13), calls=%async_computation.1 | async-start | bytes 1835008 | tf_op jit(solution)/shard_map/all_to_all | solution.py:46
  45.9 1.6 maximum_add_fusion
  49.3 5.8 %all-to-all-done.1 = bf16[16,32,896]{2,1,0:T(8,128)(2,1)S(1)} async-done(((bf16[16,32,896]{2,1,0:T(8,128)(2,1)}), bf16[16,32,896]{2,1,0:T(8,128)(2,1)S(1)}, u32[]{:S(2)}, u32[]{:S(2)}) %all-to-all-start.1) | async-done | bytes 917536 | tf_op jit(solution)/shard_map/all_to_all | solution.py:46
  55.1 3.5 %fusion.52 = f32[512,1152]{1,0:T(8,128)S(1)} fusion(bf16[512,896]{1,0:T(8,128)(2,1)S(1)} %bitcast.126, bf16[1152,896]{1,0:T(8,128)(2,1)} %pad_maximum_fusion.1), kind=kOutput, calls=%fused_computation.131 | convolution fusion | flops 1056964608 | bytes 5341184 | tf_op jit(solution)/shard_map/dot_general | solution.py:21
  58.7 1.5 fusion.51
  61.3 1.8 collective-permute-done.2
  66.6 11.7 %collective-permute-done.3 = bf16[2,64,1152]{2,1,0:T(8,128)(2,1)S(1)} collective-permute-done((bf16[2,64,1152]{2,1,0:T(8,128)(2,1)S(1)}, bf16[2,64,1152]{2,1,0:T(8,128)(2,1)S(1)}, u32[]{:S(2)}, u32[]{:S(2)}) %collective-permute-start.3) | collective-permute-done | bytes 294944 | tf_op jit(solution)/shard_map/ppermute | solution.py:27
  78.4 7.4 %collective-permute-done.7 = bf16[2,128,1152]{2,1,0:T(8,128)(2,1)S(1)} collective-permute-done((bf16[2,128,1152]{2,1,0:T(8,128)(2,1)S(1)}, bf16[2,128,1152]{2,1,0:T(8,128)(2,1)S(1)}, u32[]{:S(2)}, u32[]{:S(2)}) %collective-permute-start.7) | collective-permute-done | bytes 589856 | tf_op jit(solution)/shard_map/ppermute | solution.py:27
  85.9 2.2 collective-permute-start.8
  88.7 15.5 %collective-permute-done.8 = bf16[2,64,1152]{2,1,0:T(8,128)(2,1)S(1)} collective-permute-done((bf16[2,64,1152]{2,1,0:T(8,128)(2,1)S(1)}, bf16[2,64,1152]{2,1,0:T(8,128)(2,1)S(1)}, u32[]{:S(2)}, u32[]{:S(2)}) %collective-permute-start.8) | collective-permute-done | bytes 294944 | tf_op jit(solution)/shard_map/ppermute | solution.py:27
  104.4 3.2 %collective-permute-start.9 = (bf16[64,1152]{1,0:T(8,128)(2,1)S(1)}, bf16[64,1152]{1,0:T(8,128)(2,1)S(1)}, u32[]{:S(2)}, u32[]{:S(2)}) collective-permute-start(bf16[64,1152]{1,0:T(8,128)(2,1)S(1)} %fusion.37), channel_id=1, source_target_pairs={{0,4},{2,6},{4,0},{6,2},{1,5},{3,7},{5,1},{7,3},{8,12},{10,14},{12... | collective-permute-start | bytes 442376 | tf_op jit(solution)/shard_map/ppermute | solution.py:27
  107.7 2.3 collective-permute-start.5
  110.0 3.8 %collective-permute-done.9 = bf16[64,1152]{1,0:T(8,128)(2,1)S(1)} collective-permute-done((bf16[64,1152]{1,0:T(8,128)(2,1)S(1)}, bf16[64,1152]{1,0:T(8,128)(2,1)S(1)}, u32[]{:S(2)}, u32[]{:S(2)}) %collective-permute-start.9) | collective-permute-done | bytes 147488 | tf_op jit(solution)/shard_map/ppermute | solution.py:27
  113.8 2.7 collective-permute-start.10
  116.5 2.6 collective-permute-done.5
  119.2 6.2 %collective-permute-done.10 = bf16[128,1152]{1,0:T(8,128)(2,1)S(1)} collective-permute-done((bf16[128,1152]{1,0:T(8,128)(2,1)S(1)}, bf16[128,1152]{1,0:T(8,128)(2,1)S(1)}, u32[]{:S(2)}, u32[]{:S(2)}) %collective-permute-start.10) | collective-permute-done | bytes 294944 | tf_op jit(solution)/shard_map/ppermute | solution.py:27
  129.3 1.5 convolution_convert_fusion.1
  133.7 7.9 %all-to-all-start.2 = ((bf16[16,64,896]{2,1,0:T(8,128)(2,1)}), bf16[16,64,896]{2,1,0:T(8,128)(2,1)S(1)}, u32[]{:S(2)}, u32[]{:S(2)}) async-start(bf16[16,64,896]{2,1,0:T(8,128)(2,1)} %bitcast.25), calls=%async_computation.2 | async-start | bytes 3670016 | tf_op jit(solution)/shard_map/all_to_all | solution.py:46
  147.8 2.9 %pad_maximum_fusion.4 = bf16[16,2,32,896]{3,2,1,0:T(8,128)(2,1)} fusion(bf16[16,1,32,896]{3,2,1,0:T(8,128)(2,1)} %bitcast.128, bf16[16,1,32,896]{3,2,1,0:T(8,128)(2,1)} %bitcast.125), kind=kLoop, calls=%fused_computation.15 | loop fusion | flops 917504 | bytes 3670016 | tf_op jit(solution)/shard_map/stack | solution.py:98
  150.7 13.4 %all-to-all-done.2 = bf16[16,64,896]{2,1,0:T(8,128)(2,1)S(1)} async-done(((bf16[16,64,896]{2,1,0:T(8,128)(2,1)}), bf16[16,64,896]{2,1,0:T(8,128)(2,1)S(1)}, u32[]{:S(2)}, u32[]{:S(2)}) %all-to-all-start.2) | async-done | bytes 1835040 | tf_op jit(solution)/shard_map/all_to_all | solution.py:46
  166.3 6.8 %collective-permute-done.13 = bf16[64,896]{1,0:T(8,128)(2,1)S(1)} collective-permute-done((bf16[64,896]{1,0:T(8,128)(2,1)}, bf16[64,896]{1,0:T(8,128)(2,1)S(1)}, u32[]{:S(2)}, u32[]{:S(2)}) %collective-permute-start.13) | collective-permute-done | bytes 114720 | tf_op jit(solution)/shard_map/ppermute | solution.py:27
  174.1 1.5 broadcast_in_dim.14
  175.6 10.5 %all-to-all-start.3 = ((bf16[16,64,896]{2,1,0:T(8,128)(2,1)}), bf16[16,64,896]{2,1,0:T(8,128)(2,1)S(1)}, u32[]{:S(2)}, u32[]{:S(2)}) async-start(bf16[16,64,896]{2,1,0:T(8,128)(2,1)} %broadcast_in_dim.14), calls=%async_computation.3 | async-start | bytes 3670016 | tf_op jit(solution)/shard_map/all_to_all | solution.py:46
  188.0 13.7 %collective-permute-done.14 = bf16[1152,256]{1,0:T(8,128)(2,1)} collective-permute-done((bf16[1152,256]{1,0:T(8,128)(2,1)}, bf16[1152,256]{1,0:T(8,128)(2,1)}, u32[]{:S(2)}, u32[]{:S(2)}) %collective-permute-start.14) | collective-permute-done | bytes 589856 | tf_op jit(solution)/shard_map/ppermute | solution.py:27
  201.7 9.0 %all-to-all-done.3 = bf16[16,64,896]{2,1,0:T(8,128)(2,1)S(1)} async-done(((bf16[16,64,896]{2,1,0:T(8,128)(2,1)}), bf16[16,64,896]{2,1,0:T(8,128)(2,1)S(1)}, u32[]{:S(2)}, u32[]{:S(2)}) %all-to-all-start.3) | async-done | bytes 1835040 | tf_op jit(solution)/shard_map/all_to_all | solution.py:46
  216.0 2.0 constant_dynamic-update-slice_fusion
  219.3 2.0 multiply_reduce_fusion
  222.6 2.1 fusion.10
  225.3 2.1 collective-permute-done.16
  231.0 1.6 collective-permute-done.20
  232.7 2.4 collective-permute-done.19
  235.2 3.2 %collective-permute-start.21 = (bf16[576,128]{1,0:T(8,128)(2,1)S(1)}, bf16[576,128]{1,0:T(8,128)(2,1)S(1)}, u32[]{:S(2)}, u32[]{:S(2)}) collective-permute-start(bf16[576,128]{1,0:T(8,128)(2,1)S(1)} %fusion.36), channel_id=1, source_target_pairs={{0,4},{2,6},{4,0},{6,2},{1,5},{3,7},{5,1},{7,3},{8,12},{10,14},{12... | collective-permute-start | bytes 442376 | tf_op jit(solution)/shard_map/ppermute | solution.py:27
  239.6 5.0 %collective-permute-done.22 = f32[8,128]{1,0:T(8,128)S(1)} collective-permute-done((f32[8,128]{1,0:T(8,128)S(1)}, f32[8,128]{1,0:T(8,128)S(1)}, u32[]{:S(2)}, u32[]{:S(2)}) %collective-permute-start.22) | collective-permute-done | bytes 4128 | tf_op jit(solution)/shard_map/ppermute | solution.py:27
  244.7 2.6 collective-permute-start.23
  248.5 5.7 %collective-permute-done.23 = bf16[576,256]{1,0:T(8,128)(2,1)S(1)} collective-permute-done((bf16[576,256]{1,0:T(8,128)(2,1)S(1)}, bf16[576,256]{1,0:T(8,128)(2,1)S(1)}, u32[]{:S(2)}, u32[]{:S(2)}) %collective-permute-start.23) | collective-permute-done | bytes 294944 | tf_op jit(solution)/shard_map/ppermute | solution.py:27
  255.4 1.9 fusion.18
  257.3 1.9 fusion.16
  259.2 1.8 fusion.14
  261.0 1.8 fusion.12
  (157 shorter events, 47.7 us)
Async XLA Ops:
  0.6 16.1 %copy-start.2 = (bf16[896,576]{0,1:T(8,128)(2,1)S(1)}, bf16[896,576]{0,1:T(8,128)(2,1)}, u32[]{:S(2)}) copy-start(bf16[896,576]{0,1:T(8,128)(2,1)} %param.15) | copy-start | bytes 3096580
  0.6 16.1 %copy-start.3 = (bf16[896,576]{0,1:T(8,128)(2,1)S(1)}, bf16[896,576]{0,1:T(8,128)(2,1)}, u32[]{:S(2)}) copy-start(bf16[896,576]{0,1:T(8,128)(2,1)} %param.16) | copy-start | bytes 3096580
  0.7 16.0 %copy-start.19 = (f32[2,576]{1,0:T(2,128)S(1)}, f32[2,576]{1,0:T(2,128)}, u32[]{:S(2)}) copy-start(f32[2,576]{1,0:T(2,128)} %param.21) | copy-start | bytes 13828
  0.7 16.0 %copy-start.18 = (s32[2,576]{1,0:T(2,128)S(1)}, s32[2,576]{1,0:T(2,128)}, u32[]{:S(2)}) copy-start(s32[2,576]{1,0:T(2,128)} %param.22) | copy-start | bytes 13828
  0.7 15.9 %copy-start.17 = (s32[2,576]{1,0:T(2,128)S(1)}, s32[2,576]{1,0:T(2,128)}, u32[]{:S(2)}) copy-start(s32[2,576]{1,0:T(2,128)} %param.23) | copy-start | bytes 13828
  0.7 15.9 %collective-permute-start = (bf16[32,896]{1,0:T(8,128)(2,1)}, bf16[32,896]{1,0:T(8,128)(2,1)S(1)}, u32[]{:S(2)}, u32[]{:S(2)}) collective-permute-start(bf16[32,896]{1,0:T(8,128)(2,1)} %param.14), channel_id=1, source_target_pairs={{0,8},{8,0},{1,9},{9,1},{2,10},{10,2},{3,11},{11,3},{4,12},{12,4},... | collective-permute-start | bytes 172040 | tf_op jit(solution)/shard_map/ppermute | solution.py:27
  7.7 21.6 %all-to-all-start = ((bf16[16,32,896]{2,1,0:T(8,128)(2,1)}), bf16[16,32,896]{2,1,0:T(8,128)(2,1)S(1)}, u32[]{:S(2)}, u32[]{:S(2)}) async-start(bf16[16,32,896]{2,1,0:T(8,128)(2,1)} %broadcast_in_dim.12), calls=%async_computation | async-start | bytes 1835008 | tf_op jit(solution)/shard_map/all_to_all | solution.py:46
  29.3 3.5 %copy-start.4 = (bf16[16,32,896]{2,1,0:T(8,128)(2,1)}, bf16[16,32,896]{2,1,0:T(8,128)(2,1)S(1)}, u32[]{:S(2)}) copy-start(bf16[16,32,896]{2,1,0:T(8,128)(2,1)S(1)} %all-to-all-done) | copy-start | bytes 2752516
  29.3 3.5 %copy-start.7 = (bf16[1152,896]{1,0:T(8,128)(2,1)S(1)}, bf16[1152,896]{1,0:T(8,128)(2,1)}, u32[]{:S(2)}) copy-start(bf16[1152,896]{1,0:T(8,128)(2,1)} %pad_maximum_fusion) | copy-start | bytes 6193156
  36.2 9.6 %collective-permute-start.1 = (bf16[2,256,1152]{2,1,0:T(8,128)(2,1)}, bf16[2,256,1152]{2,1,0:T(8,128)(2,1)}, u32[]{:S(2)}, u32[]{:S(2)}) collective-permute-start(bf16[2,256,1152]{2,1,0:T(8,128)(2,1)} %pad_maximum_fusion.5), channel_id=1, source_target_pairs={{0,1},{1,0},{2,3},{3,2},{4,5},{5,4},{6,7},{7,6},{8,9},{9,8},{10,11... | collective-permute-start | bytes 3538952 | tf_op jit(solution)/shard_map/ppermute | solution.py:27
  37.6 8.2 %copy-start.11 = (f32[512,1152]{1,0:T(8,128)S(1)}, f32[512,1152]{1,0:T(8,128)}, u32[]{:S(2)}) copy-start(f32[512,1152]{1,0:T(8,128)} %copy-done.10) | copy-start | bytes 7077892
  37.6 17.5 %all-to-all-start.1 = ((bf16[16,32,896]{2,1,0:T(8,128)(2,1)}), bf16[16,32,896]{2,1,0:T(8,128)(2,1)S(1)}, u32[]{:S(2)}, u32[]{:S(2)}) async-start(bf16[16,32,896]{2,1,0:T(8,128)(2,1)} %broadcast_in_dim.13), calls=%async_computation.1 | async-start | bytes 1835008 | tf_op jit(solution)/shard_map/all_to_all | solution.py:46
  48.3 14.8 %collective-permute-start.2 = (bf16[2,128,1152]{2,1,0:T(8,128)(2,1)}, bf16[2,128,1152]{2,1,0:T(8,128)(2,1)}, u32[]{:S(2)}, u32[]{:S(2)}) collective-permute-start(bf16[2,128,1152]{2,1,0:T(8,128)(2,1)} %slice.332), channel_id=1, source_target_pairs={{0,2},{2,0},{4,6},{6,4},{1,3},{3,1},{5,7},{7,5},{8,10},{10,8},{12,... | collective-permute-start | bytes 1769480 | tf_op jit(solution)/shard_map/ppermute | solution.py:27
  55.1 3.5 %copy-start.5 = (bf16[16,32,896]{2,1,0:T(8,128)(2,1)}, bf16[16,32,896]{2,1,0:T(8,128)(2,1)S(1)}, u32[]{:S(2)}) copy-start(bf16[16,32,896]{2,1,0:T(8,128)(2,1)S(1)} %all-to-all-done.1) | copy-start | bytes 2752516
  55.1 3.5 %copy-start.8 = (bf16[1152,896]{1,0:T(8,128)(2,1)S(1)}, bf16[1152,896]{1,0:T(8,128)(2,1)}, u32[]{:S(2)}) copy-start(bf16[1152,896]{1,0:T(8,128)(2,1)} %pad_maximum_fusion) | copy-start | bytes 6193156
  60.5 5.1 %collective-permute-start.6 = (bf16[2,256,1152]{2,1,0:T(8,128)(2,1)S(1)}, bf16[2,256,1152]{2,1,0:T(8,128)(2,1)S(1)}, u32[]{:S(2)}, u32[]{:S(2)}) collective-permute-start(bf16[2,256,1152]{2,1,0:T(8,128)(2,1)S(1)} %pad_maximum_fusion.6), channel_id=1, source_target_pairs={{0,1},{1,0},{2,3},{3,2},{4,5},{5,4},{6,7},{7,6},{8,9},{9,8},{10,11... | collective-permute-start | bytes 3538952 | tf_op jit(solution)/shard_map/ppermute | solution.py:27
  64.3 2.3 copy-start.20
  64.3 14.0 %collective-permute-start.3 = (bf16[2,64,1152]{2,1,0:T(8,128)(2,1)S(1)}, bf16[2,64,1152]{2,1,0:T(8,128)(2,1)S(1)}, u32[]{:S(2)}, u32[]{:S(2)}) collective-permute-start(bf16[2,64,1152]{2,1,0:T(8,128)(2,1)S(1)} %slice.334), channel_id=1, source_target_pairs={{0,4},{2,6},{4,0},{6,2},{1,5},{3,7},{5,1},{7,3},{8,12},{10,14},{12... | collective-permute-start | bytes 884744 | tf_op jit(solution)/shard_map/ppermute | solution.py:27
  65.8 19.9 %collective-permute-start.7 = (bf16[2,128,1152]{2,1,0:T(8,128)(2,1)S(1)}, bf16[2,128,1152]{2,1,0:T(8,128)(2,1)S(1)}, u32[]{:S(2)}, u32[]{:S(2)}) collective-permute-start(bf16[2,128,1152]{2,1,0:T(8,128)(2,1)S(1)} %slice.331), channel_id=1, source_target_pairs={{0,2},{2,0},{4,6},{6,4},{1,3},{3,1},{5,7},{7,5},{8,10},{10,8},{12,... | collective-permute-start | bytes 1769480 | tf_op jit(solution)/shard_map/ppermute | solution.py:27
  85.9 30.5 %copy-start.21 = (f32[896]{0:T(1024)S(1)}, f32[896]{0:T(1024)}, u32[]{:S(2)}) copy-start(f32[896]{0:T(1024)} %param.24) | copy-start | bytes 10756
  85.9 30.5 %copy-start.22 = (s32[896]{0:T(1024)S(1)}, s32[896]{0:T(1024)}, u32[]{:S(2)}) copy-start(s32[896]{0:T(1024)} %param.26) | copy-start | bytes 10756
  85.9 18.4 %collective-permute-start.8 = (bf16[2,64,1152]{2,1,0:T(8,128)(2,1)S(1)}, bf16[2,64,1152]{2,1,0:T(8,128)(2,1)S(1)}, u32[]{:S(2)}, u32[]{:S(2)}) collective-permute-start(bf16[2,64,1152]{2,1,0:T(8,128)(2,1)S(1)} %slice.333), channel_id=1, source_target_pairs={{0,4},{2,6},{4,0},{6,2},{1,5},{3,7},{5,1},{7,3},{8,12},{10,14},{12... | collective-permute-start | bytes 884744 | tf_op jit(solution)/shard_map/ppermute | solution.py:27
  88.2 19.4 %collective-permute-start.4 = (bf16[64,1152]{1,0:T(8,128)(2,1)S(1)}, bf16[64,1152]{1,0:T(8,128)(2,1)S(1)}, u32[]{:S(2)}, u32[]{:S(2)}) collective-permute-start(bf16[64,1152]{1,0:T(8,128)(2,1)S(1)} %fusion.41), channel_id=1, source_target_pairs={{0,4},{2,6},{4,0},{6,2},{1,5},{3,7},{5,1},{7,3},{8,12},{10,14},{12... | collective-permute-start | bytes 442376 | tf_op jit(solution)/shard_map/ppermute | solution.py:27
  104.4 9.3 %collective-permute-start.9 = (bf16[64,1152]{1,0:T(8,128)(2,1)S(1)}, bf16[64,1152]{1,0:T(8,128)(2,1)S(1)}, u32[]{:S(2)}, u32[]{:S(2)}) collective-permute-start(bf16[64,1152]{1,0:T(8,128)(2,1)S(1)} %fusion.37), channel_id=1, source_target_pairs={{0,4},{2,6},{4,0},{6,2},{1,5},{3,7},{5,1},{7,3},{8,12},{10,14},{12... | collective-permute-start | bytes 442376 | tf_op jit(solution)/shard_map/ppermute | solution.py:27
  107.7 11.4 %collective-permute-start.5 = (bf16[128,1152]{1,0:T(8,128)(2,1)S(1)}, bf16[128,1152]{1,0:T(8,128)(2,1)S(1)}, u32[]{:S(2)}, u32[]{:S(2)}) collective-permute-start(bf16[128,1152]{1,0:T(8,128)(2,1)S(1)} %pad_maximum_fusion.14), channel_id=1, source_target_pairs={{0,2},{2,0},{4,6},{6,4},{1,3},{3,1},{5,7},{7,5},{8,10},{10,8},{12,... | collective-permute-start | bytes 884744 | tf_op jit(solution)/shard_map/ppermute | solution.py:27
  113.8 11.6 %collective-permute-start.10 = (bf16[128,1152]{1,0:T(8,128)(2,1)S(1)}, bf16[128,1152]{1,0:T(8,128)(2,1)S(1)}, u32[]{:S(2)}, u32[]{:S(2)}) collective-permute-start(bf16[128,1152]{1,0:T(8,128)(2,1)S(1)} %pad_maximum_fusion.15), channel_id=1, source_target_pairs={{0,2},{2,0},{4,6},{6,4},{1,3},{3,1},{5,7},{7,5},{8,10},{10,8},{12,... | collective-permute-start | bytes 884744 | tf_op jit(solution)/shard_map/ppermute | solution.py:27
  119.1 7.7 %copy-start.1 = (bf16[576,896]{1,0:T(8,128)(2,1)S(1)}, bf16[576,896]{1,0:T(8,128)(2,1)}, u32[]{:S(2)}) copy-start(bf16[576,896]{1,0:T(8,128)(2,1)} %param.17) | copy-start | bytes 3096580
  119.1 7.7 %copy-start.13 = (bf16[576,896]{1,0:T(8,128)(2,1)S(1)}, bf16[576,896]{1,0:T(8,128)(2,1)}, u32[]{:S(2)}) copy-start(bf16[576,896]{1,0:T(8,128)(2,1)} %param.20) | copy-start | bytes 3096580
  125.6 3.7 %copy-start.6 = (bf16[8,2,32,1152]{3,2,1,0:T(8,128)(2,1)}, bf16[8,2,32,1152]{3,2,1,0:T(8,128)(2,1)S(1)}, u32[]{:S(2)}) copy-start(bf16[8,2,32,1152]{3,2,1,0:T(8,128)(2,1)S(1)} %pad_maximum_fusion.7) | copy-start | bytes 3538948
  125.6 5.1 %collective-permute-start.11 = (bf16[512,1152]{1,0:T(8,128)(2,1)S(1)}, bf16[512,1152]{1,0:T(8,128)(2,1)S(1)}, u32[]{:S(2)}, u32[]{:S(2)}) collective-permute-start(bf16[512,1152]{1,0:T(8,128)(2,1)S(1)} %bitcast.129), channel_id=1, source_target_pairs={{0,1},{1,0},{2,3},{3,2},{4,5},{5,4},{6,7},{7,6},{8,9},{9,8},{10,11... | collective-permute-start | bytes 3538952 | tf_op jit(solution)/shard_map/ppermute | solution.py:27
  133.7 30.4 %all-to-all-start.2 = ((bf16[16,64,896]{2,1,0:T(8,128)(2,1)}), bf16[16,64,896]{2,1,0:T(8,128)(2,1)S(1)}, u32[]{:S(2)}, u32[]{:S(2)}) async-start(bf16[16,64,896]{2,1,0:T(8,128)(2,1)} %bitcast.25), calls=%async_computation.2 | async-start | bytes 3670016 | tf_op jit(solution)/shard_map/all_to_all | solution.py:46
  143.7 4.1 %copy-start.16 = (f32[1024]{0:T(1024)S(1)}, f32[1024]{0:T(1024)}, u32[]{:S(2)}) copy-start(f32[1024]{0:T(1024)} %param.27) | copy-start | bytes 12292
  147.0 18.1 %collective-permute-start.12 = (bf16[1152,128]{1,0:T(8,128)(2,1)S(1)}, bf16[1152,128]{1,0:T(8,128)(2,1)S(1)}, u32[]{:S(2)}, u32[]{:S(2)}) collective-permute-start(bf16[1152,128]{1,0:T(8,128)(2,1)S(1)} %pad_maximum_fusion.16), channel_id=1, source_target_pairs={{0,4},{2,6},{4,0},{6,2},{1,5},{3,7},{5,1},{7,3},{8,12},{10,14},{12... | collective-permute-start | bytes 884744 | tf_op jit(solution)/shard_map/ppermute | solution.py:27
  165.0 8.1 %collective-permute-start.13 = (bf16[64,896]{1,0:T(8,128)(2,1)}, bf16[64,896]{1,0:T(8,128)(2,1)S(1)}, u32[]{:S(2)}, u32[]{:S(2)}) collective-permute-start(bf16[64,896]{1,0:T(8,128)(2,1)} %reduce_sum.21), channel_id=1, source_target_pairs={{0,8},{8,0},{1,9},{9,1},{2,10},{10,2},{3,11},{11,3},{4,12},{12,4},... | collective-permute-start | bytes 344072 | tf_op jit(solution)/shard_map/ppermute | solution.py:27
  175.6 35.0 %all-to-all-start.3 = ((bf16[16,64,896]{2,1,0:T(8,128)(2,1)}), bf16[16,64,896]{2,1,0:T(8,128)(2,1)S(1)}, u32[]{:S(2)}, u32[]{:S(2)}) async-start(bf16[16,64,896]{2,1,0:T(8,128)(2,1)} %broadcast_in_dim.14), calls=%async_computation.3 | async-start | bytes 3670016 | tf_op jit(solution)/shard_map/all_to_all | solution.py:46
  187.1 14.5 %collective-permute-start.14 = (bf16[1152,256]{1,0:T(8,128)(2,1)}, bf16[1152,256]{1,0:T(8,128)(2,1)}, u32[]{:S(2)}, u32[]{:S(2)}) collective-permute-start(bf16[1152,256]{1,0:T(8,128)(2,1)} %pad_maximum_fusion.12), channel_id=1, source_target_pairs={{0,2},{2,0},{4,6},{6,4},{1,3},{3,1},{5,7},{7,5},{8,10},{10,8},{12,... | collective-permute-start | bytes 1769480 | tf_op jit(solution)/shard_map/ppermute | solution.py:27
  214.4 3.7 %collective-permute-start.15 = (bf16[576,512]{1,0:T(8,128)(2,1)}, bf16[576,512]{1,0:T(8,128)(2,1)S(1)}, u32[]{:S(2)}, u32[]{:S(2)}) collective-permute-start(bf16[576,512]{1,0:T(8,128)(2,1)} %slice.330), channel_id=1, source_target_pairs={{0,1},{1,0},{2,3},{3,2},{4,5},{5,4},{6,7},{7,6},{8,9},{9,8},{10,11... | collective-permute-start | bytes 1769480 | tf_op jit(solution)/shard_map/ppermute | solution.py:27
  218.0 9.4 %collective-permute-start.18 = (bf16[1152,512]{1,0:T(8,128)(2,1)}, bf16[1152,512]{1,0:T(8,128)(2,1)}, u32[]{:S(2)}, u32[]{:S(2)}) collective-permute-start(bf16[1152,512]{1,0:T(8,128)(2,1)} %constant_dynamic-update-slice_fusion), channel_id=1, source_target_pairs={{0,1},{1,0},{2,3},{3,2},{4,5},{5,4},{6,7},{7,6},{8,9},{9,8},{10,11... | collective-permute-start | bytes 3538952 | tf_op jit(solution)/shard_map/ppermute | solution.py:27
  219.2 8.1 %collective-permute-start.16 = (bf16[576,256]{1,0:T(8,128)(2,1)S(1)}, bf16[576,256]{1,0:T(8,128)(2,1)S(1)}, u32[]{:S(2)}, u32[]{:S(2)}) collective-permute-start(bf16[576,256]{1,0:T(8,128)(2,1)S(1)} %fusion.32), channel_id=1, source_target_pairs={{0,2},{2,0},{4,6},{6,4},{1,3},{3,1},{5,7},{7,5},{8,10},{10,8},{12,... | collective-permute-start | bytes 884744 | tf_op jit(solution)/shard_map/ppermute | solution.py:27
  222.0 8.1 %copy-start.15 = (bf16[512,1152]{1,0:T(8,128)(2,1)S(1)}, bf16[512,1152]{1,0:T(8,128)(2,1)}, u32[]{:S(2)}) copy-start(bf16[512,1152]{1,0:T(8,128)(2,1)} %copy-done.14) | copy-start | bytes 3538948
  222.0 2.7 collective-permute-start.17
  228.6 6.5 %collective-permute-start.19 = (bf16[576,128]{1,0:T(8,128)(2,1)S(1)}, bf16[576,128]{1,0:T(8,128)(2,1)S(1)}, u32[]{:S(2)}, u32[]{:S(2)}) collective-permute-start(bf16[576,128]{1,0:T(8,128)(2,1)S(1)} %slice.335), channel_id=1, source_target_pairs={{0,4},{2,6},{4,0},{6,2},{1,5},{3,7},{5,1},{7,3},{8,12},{10,14},{12... | collective-permute-start | bytes 442376 | tf_op jit(solution)/shard_map/ppermute | solution.py:27
  229.1 3.6 %collective-permute-start.20 = (f32[8,128]{1,0:T(8,128)S(1)}, f32[8,128]{1,0:T(8,128)S(1)}, u32[]{:S(2)}, u32[]{:S(2)}) collective-permute-start(f32[8,128]{1,0:T(8,128)S(1)} %broadcast_add_fusion), channel_id=1, source_target_pairs={{0,2},{2,0},{4,6},{6,4},{1,3},{3,1},{5,7},{7,5},{8,10},{10,8},{12,... | collective-permute-start | bytes 12296 | tf_op jit(solution)/shard_map/ppermute | solution.py:27
  235.2 20.3 %copy-start = (bf16[16,2,32,896]{3,2,1,0:T(8,128)(2,1)S(1)}, bf16[16,2,32,896]{3,2,1,0:T(8,128)(2,1)}, u32[]{:S(2)}) copy-start(bf16[16,2,32,896]{3,2,1,0:T(8,128)(2,1)} %pad_maximum_fusion.4) | copy-start | bytes 5505028
  235.2 9.5 %collective-permute-start.21 = (bf16[576,128]{1,0:T(8,128)(2,1)S(1)}, bf16[576,128]{1,0:T(8,128)(2,1)S(1)}, u32[]{:S(2)}, u32[]{:S(2)}) collective-permute-start(bf16[576,128]{1,0:T(8,128)(2,1)S(1)} %fusion.36), channel_id=1, source_target_pairs={{0,4},{2,6},{4,0},{6,2},{1,5},{3,7},{5,1},{7,3},{8,12},{10,14},{12... | collective-permute-start | bytes 442376 | tf_op jit(solution)/shard_map/ppermute | solution.py:27
  238.4 6.3 %collective-permute-start.22 = (f32[8,128]{1,0:T(8,128)S(1)}, f32[8,128]{1,0:T(8,128)S(1)}, u32[]{:S(2)}, u32[]{:S(2)}) collective-permute-start(f32[8,128]{1,0:T(8,128)S(1)} %add.158), channel_id=1, source_target_pairs={{0,4},{2,6},{4,0},{6,2},{1,5},{3,7},{5,1},{7,3},{8,12},{10,14},{12... | collective-permute-start | bytes 12296 | tf_op jit(solution)/shard_map/ppermute | solution.py:27
  244.7 9.5 %collective-permute-start.23 = (bf16[576,256]{1,0:T(8,128)(2,1)S(1)}, bf16[576,256]{1,0:T(8,128)(2,1)S(1)}, u32[]{:S(2)}, u32[]{:S(2)}) collective-permute-start(bf16[576,256]{1,0:T(8,128)(2,1)S(1)} %pad_maximum_fusion.17), channel_id=1, source_target_pairs={{0,2},{2,0},{4,6},{6,4},{1,3},{3,1},{5,7},{7,5},{8,10},{10,8},{12,... | collective-permute-start | bytes 884744 | tf_op jit(solution)/shard_map/ppermute | solution.py:27
  254.3 4.9 %collective-permute-start.24 = (bf16[576,512]{1,0:T(8,128)(2,1)S(1)}, bf16[576,512]{1,0:T(8,128)(2,1)S(1)}, u32[]{:S(2)}, u32[]{:S(2)}) collective-permute-start(bf16[576,512]{1,0:T(8,128)(2,1)S(1)} %pad_maximum_fusion.13), channel_id=1, source_target_pairs={{0,1},{1,0},{2,3},{3,2},{4,5},{5,4},{6,7},{7,6},{8,9},{9,8},{10,11... | collective-permute-start | bytes 1769480 | tf_op jit(solution)/shard_map/ppermute | solution.py:27
  (4 other events, 6.3 us)

commit v2 on v1

--- a/solution.py
+++ b/solution.py
@@ -86,11 +86,6 @@
 
 def added(value, axis, bit):
     return value + flipped(value, axis, bit)
-
-
-def gathered_half(own):
-    pair = joined(own, flipped(own, Z, 2))
-    return joined(pair, flipped(pair, Z, 1))
 
 
 def merged(first, second):
@@ -185,11 +180,16 @@
         given = own[:, 2 * rows :].astype(BF)
         if k == 0:
             planes[1], _ = together(planes[1], given)
-        kept = own[:, : 2 * rows] + flipped(given, Z, 1)
-        share = kept[:, :rows] + flipped(kept[:, rows:].astype(BF), Z, 2)
+        received = flipped(given, Z, 1)
+        kept = own[:, : 2 * rows] + received
+        received = flipped(kept[:, rows:].astype(BF), Z, 2)
+        share = kept[:, :rows] + received
         shares.append(share)
         both = (jax.nn.silu(share[0]) * share[1]).astype(BF)
-        near_planes.append(gathered_half(both))
+        received = flipped(both, Z, 2)
+        pair = joined(both, received)
+        received = flipped(pair, Z, 1)
+        near_planes.append(joined(pair, received))
     near = merged(*near_planes)
     far = flipped(near, C, 1)
 
@@ -210,9 +210,7 @@
     terms = joined(
         product(near, downs, 1, 0).astype(BF), product(far, downs, 1, 0).astype(BF)
     )
-    partial, received, all_tokens = together(
-        scatter_plane(terms).astype(BF), flipped(factors, Z, 2), all_tokens
-    )
+    partial, received = together(scatter_plane(terms).astype(BF), flipped(factors, Z, 2))
     pair = beside(factors, received)
     residual = partial.astype(F32) + halves_swapped(flipped(partial, H, 1)).astype(F32)
     pair_grad = (2.0 * (row_weight[:, None] * residual)).astype(BF)
@@ -238,29 +236,33 @@
         product(near[:, hidden:], out_grad[:half], 0, 0),
     )
     own = (kept[:, :rows] + received).astype(BF)
-    received, loss, grad_down = together(
+    received, loss, grad_down, near_gate, near_up = together(
         flipped(own, Z, 2),
         added(loss, Z, 2),
         (near_down + product(far[:, hidden:], out_grad[half:], 0, 0)).astype(BF),
+        near_factors[:hidden],
+        near_factors[hidden:],
     )
     pair = beside(own, received)
-    near_grad = beside(pair, flipped(pair, Z, 1))
+    received, far_gate, far_up = together(
+        flipped(pair, Z, 1), far_factors[:hidden], far_factors[hidden:]
+    )
+    near_grad = beside(pair, received)
     far_grad = flipped(near_grad, C, 1)
 
-    def weight_grad(first):
-        def part(grad, factor, rows):
-            scaled = grad.astype(F32) * factor[first : first + hidden]
-            return product(scaled.astype(BF), rows, 1, 0)
-
-        return part(near_grad, near_factors, all_tokens[:half]), lambda: part(
-            far_grad, far_factors, all_tokens[half:]
-        )
-
-    gate_part, gate_rest = weight_grad(0)
-    up_part, up_rest = weight_grad(hidden)
-    far_grad, gate_part, up_part = together(far_grad, gate_part, up_part)
-    grad_gate = (gate_part + gate_rest()).astype(BF)
-    grad_up = (up_part + up_rest()).astype(BF)
+    def weight_part(grad, factor, rows):
+        return product((grad.astype(F32) * factor).astype(BF), rows, 1, 0)
+
+    near_tokens, far_tokens = all_tokens[:half], all_tokens[half:]
+    far_grad, gate_part, up_part = together(
+        far_grad,
+        weight_part(near_grad, near_gate, near_tokens),
+        weight_part(near_grad, near_up, near_tokens),
+    )
+    gate_rest = weight_part(far_grad, far_gate, far_tokens)
+    up_rest = weight_part(far_grad, far_up, far_tokens)
+    grad_gate = (gate_part + gate_rest).astype(BF)
+    grad_up = (up_part + up_rest).astype(BF)
     loss_value = loss[0, 0] / (total_rows * D)
     return (loss_value, grad_gate.T, grad_up.T, grad_down)
 

time: 271 us -> 262 us (0.967)
  matrix products: 24.8 us -> 19.5 us
  waiting for transfers between devices: 120 us -> 125 us
  other arithmetic: 32.5 us -> 27.8 us
  local copies, waits for them, and re-layouts: 17.9 us -> 14.3 us
    dot_general x13, matrix products: 24.8 us -> 19.5 us  [product(): lax.dot_general(left, right, (((left_dim,), (right_dim,)), ((), ())), pre...]
    all_to_all x4, waiting for transfers between devices: 33.9 us -> 36.7 us  [exchange(): lax.all_to_all(blocks, (X, Y, H, Z, C), 0, 0, axis_index_groups=plane_gro...]
  transfers between devices with their start and end apart: 29 -> 29, of which waited for: 18 -> 19; matrix products, arithmetic and copies ran while one was open for 19% -> 17% of each run, Pallas kernels for 0% -> 0%
where the time goes in v2:
time: 262 us; the launch traced here: 257 us
  waiting for transfers between devices  125 us (48%)
  starting transfers between devices  67.7 us (26%)
  other arithmetic  27.8 us (11%)
  matrix products  19.5 us (7%)
  local copies, waits for them, and re-layouts  14.3 us (5%)
  between operations  3.16 us (1%)
    ppermute x25, waiting for transfers between devices, flipped(): return lax.ppermute(value, axis, [(i, i ^ bit) for i in range(SIZE[axis])])  88.2 us
    all_to_all x4, waiting for transfers between devices, exchange(): lax.all_to_all(blocks, (X, Y, H, Z, C), 0, 0, axis_index_groups=plane_gro...  36.7 us
    all_to_all x4, starting transfers between devices, exchange(): lax.all_to_all(blocks, (X, Y, H, Z, C), 0, 0, axis_index_groups=plane_gro...  34.1 us
    ppermute x25, starting transfers between devices, flipped(): return lax.ppermute(value, axis, [(i, i ^ bit) for i in range(SIZE[axis])])  33.5 us
    dot_general x13, matrix products, product(): lax.dot_general(left, right, (((left_dim,), (right_dim,)), ((), ())), pre...  19.5 us
  transfers between devices with their start and end apart: 29, of which 19 were waited for; matrix products, arithmetic and copies ran while one was open for 17% of the time, Pallas kernels for 0%

profile of v2, /device:TPU:65, one launch (start us, length us, event | category | flops | bytes accessed | tf_op | source)
XLA Modules:
  0.0 257.4 jit_solution(13533354657555559770)
XLA Ops:
  0.7 5.2 %collective-permute-start = (bf16[32,896]{1,0:T(8,128)(2,1)}, bf16[32,896]{1,0:T(8,128)(2,1)S(1)}, u32[]{:S(2)}, u32[]{:S(2)}) collective-permute-start(bf16[32,896]{1,0:T(8,128)(2,1)} %param.14), channel_id=1, source_target_pairs={{0,8},{8,0},{1,9},{9,1},{2,10},{10,2},{3,11},{11,3},{4,12},{12,4},... | collective-permute-start | bytes 172040 | tf_op jit(solution)/shard_map/ppermute | solution.py:27
  5.9 1.8 broadcast_in_dim.12
  7.7 8.9 %all-to-all-start = ((bf16[16,32,896]{2,1,0:T(8,128)(2,1)}), bf16[16,32,896]{2,1,0:T(8,128)(2,1)S(1)}, u32[]{:S(2)}, u32[]{:S(2)}) async-start(bf16[16,32,896]{2,1,0:T(8,128)(2,1)} %broadcast_in_dim.12), calls=%async_computation | async-start | bytes 1835008 | tf_op jit(solution)/shard_map/all_to_all | solution.py:46
  16.7 3.9 %fusion.6 = (bf16[576,896]{1,0:T(8,128)(2,1)S(1)}, bf16[576,896]{1,0:T(8,128)(2,1)S(1)}) fusion(f32[576]{0:T(1024)S(1)} %get-tuple-element.85, bf16[896,576]{0,1:T(8,128)(2,1)} %param.18, bf16[896,576]{0,1:T(8,128)(2,1)S(1)} %copy-done.1, f32[576]{0:T(1024)S(1)} %get-tuple-element.83, f32[576]{0:T(1024)S(1)} %get-tuple-element.81, ...), kind=kLoop, calls=%fused_computation.45 | loop fusion | flops 17547264 | bytes 6206976 | tf_op jit(solution)/shard_map/transpose | solution.py:166
  20.6 1.5 pad_maximum_fusion
  22.1 1.6 pad_maximum_fusion.1
  23.7 5.6 %all-to-all-done = bf16[16,32,896]{2,1,0:T(8,128)(2,1)S(1)} async-done(((bf16[16,32,896]{2,1,0:T(8,128)(2,1)}), bf16[16,32,896]{2,1,0:T(8,128)(2,1)S(1)}, u32[]{:S(2)}, u32[]{:S(2)}) %all-to-all-start) | async-done | bytes 917536 | tf_op jit(solution)/shard_map/all_to_all | solution.py:46
  29.3 3.5 %convolution_bitcast_fusion = f32[512,1152]{1,0:T(8,128)S(1)} fusion(bf16[1152,896]{1,0:T(8,128)(2,1)} %pad_maximum_fusion.1, bf16[512,896]{1,0:T(8,128)(2,1)S(1)} %bitcast.128), kind=kOutput, calls=%fused_computation.1 | convolution fusion | flops 1056964608 | bytes 5341184 | tf_op jit(solution)/shard_map/dot_general | solution.py:21
  32.9 1.5 convolution_bitcast_fusion.1
  34.5 1.4 pad_maximum_fusion.4
  37.6 6.8 %all-to-all-start.1 = ((bf16[16,32,896]{2,1,0:T(8,128)(2,1)}), bf16[16,32,896]{2,1,0:T(8,128)(2,1)S(1)}, u32[]{:S(2)}, u32[]{:S(2)}) async-start(bf16[16,32,896]{2,1,0:T(8,128)(2,1)} %broadcast_in_dim.13), calls=%async_computation.1 | async-start | bytes 1835008 | tf_op jit(solution)/shard_map/all_to_all | solution.py:46
  44.4 1.3 slice_bitcast_fusion.2
  45.9 1.6 maximum_add_fusion
  49.4 5.8 %all-to-all-done.1 = bf16[16,32,896]{2,1,0:T(8,128)(2,1)S(1)} async-done(((bf16[16,32,896]{2,1,0:T(8,128)(2,1)}), bf16[16,32,896]{2,1,0:T(8,128)(2,1)S(1)}, u32[]{:S(2)}, u32[]{:S(2)}) %all-to-all-start.1) | async-done | bytes 917536 | tf_op jit(solution)/shard_map/all_to_all | solution.py:46
  55.2 3.5 %fusion.47 = f32[512,1152]{1,0:T(8,128)S(1)} fusion(bf16[512,896]{1,0:T(8,128)(2,1)S(1)} %bitcast.131, bf16[1152,896]{1,0:T(8,128)(2,1)} %pad_maximum_fusion.1), kind=kOutput, calls=%fused_computation.128 | convolution fusion | flops 1056964608 | bytes 5341184 | tf_op jit(solution)/shard_map/dot_general | solution.py:21
  58.7 1.5 fusion.46
  61.4 1.8 collective-permute-done.2
  64.4 1.2 collective-permute-start.3
  66.6 11.7 %collective-permute-done.3 = bf16[2,64,1152]{2,1,0:T(8,128)(2,1)S(1)} collective-permute-done((bf16[2,64,1152]{2,1,0:T(8,128)(2,1)S(1)}, bf16[2,64,1152]{2,1,0:T(8,128)(2,1)S(1)}, u32[]{:S(2)}, u32[]{:S(2)}) %collective-permute-start.3) | collective-permute-done | bytes 294944 | tf_op jit(solution)/shard_map/ppermute | solution.py:27
  78.4 7.4 %collective-permute-done.7 = bf16[2,128,1152]{2,1,0:T(8,128)(2,1)S(1)} collective-permute-done((bf16[2,128,1152]{2,1,0:T(8,128)(2,1)S(1)}, bf16[2,128,1152]{2,1,0:T(8,128)(2,1)S(1)}, u32[]{:S(2)}, u32[]{:S(2)}) %collective-permute-start.7) | collective-permute-done | bytes 589856 | tf_op jit(solution)/shard_map/ppermute | solution.py:27
  85.9 2.2 collective-permute-start.8
  88.8 15.5 %collective-permute-done.8 = bf16[2,64,1152]{2,1,0:T(8,128)(2,1)S(1)} collective-permute-done((bf16[2,64,1152]{2,1,0:T(8,128)(2,1)S(1)}, bf16[2,64,1152]{2,1,0:T(8,128)(2,1)S(1)}, u32[]{:S(2)}, u32[]{:S(2)}) %collective-permute-start.8) | collective-permute-done | bytes 294944 | tf_op jit(solution)/shard_map/ppermute | solution.py:27
  104.5 3.2 %collective-permute-start.9 = (bf16[64,1152]{1,0:T(8,128)(2,1)S(1)}, bf16[64,1152]{1,0:T(8,128)(2,1)S(1)}, u32[]{:S(2)}, u32[]{:S(2)}) collective-permute-start(bf16[64,1152]{1,0:T(8,128)(2,1)S(1)} %fusion.30), channel_id=1, source_target_pairs={{0,4},{2,6},{4,0},{6,2},{1,5},{3,7},{5,1},{7,3},{8,12},{10,14},{12... | collective-permute-start | bytes 442376 | tf_op jit(solution)/shard_map/ppermute | solution.py:27
  107.7 2.3 collective-permute-start.5
  110.0 3.8 %collective-permute-done.9 = bf16[64,1152]{1,0:T(8,128)(2,1)S(1)} collective-permute-done((bf16[64,1152]{1,0:T(8,128)(2,1)S(1)}, bf16[64,1152]{1,0:T(8,128)(2,1)S(1)}, u32[]{:S(2)}, u32[]{:S(2)}) %collective-permute-start.9) | collective-permute-done | bytes 147488 | tf_op jit(solution)/shard_map/ppermute | solution.py:27
  113.8 2.7 %collective-permute-start.10 = (bf16[128,1152]{1,0:T(8,128)(2,1)S(1)}, bf16[128,1152]{1,0:T(8,128)(2,1)S(1)}, u32[]{:S(2)}, u32[]{:S(2)}) collective-permute-start(bf16[128,1152]{1,0:T(8,128)(2,1)S(1)} %pad_maximum_fusion.15), channel_id=1, source_target_pairs={{0,2},{2,0},{4,6},{6,4},{1,3},{3,1},{5,7},{7,5},{8,10},{10,8},{12,... | collective-permute-start | bytes 884744 | tf_op jit(solution)/shard_map/ppermute | solution.py:27
  116.5 2.6 %collective-permute-done.5 = bf16[128,1152]{1,0:T(8,128)(2,1)S(1)} collective-permute-done((bf16[128,1152]{1,0:T(8,128)(2,1)S(1)}, bf16[128,1152]{1,0:T(8,128)(2,1)S(1)}, u32[]{:S(2)}, u32[]{:S(2)}) %collective-permute-start.5) | collective-permute-done | bytes 294944 | tf_op jit(solution)/shard_map/ppermute | solution.py:27
  119.2 6.2 %collective-permute-done.10 = bf16[128,1152]{1,0:T(8,128)(2,1)S(1)} collective-permute-done((bf16[128,1152]{1,0:T(8,128)(2,1)S(1)}, bf16[128,1152]{1,0:T(8,128)(2,1)S(1)}, u32[]{:S(2)}, u32[]{:S(2)}) %collective-permute-start.10) | collective-permute-done | bytes 294944 | tf_op jit(solution)/shard_map/ppermute | solution.py:27
  125.6 1.2 collective-permute-start.11
  129.3 1.5 convolution_convert_fusion.1
  130.8 1.5 convolution_convert_fusion
  132.3 1.4 pad_maximum_fusion.3
  133.7 7.9 %all-to-all-start.2 = ((bf16[16,64,896]{2,1,0:T(8,128)(2,1)}), bf16[16,64,896]{2,1,0:T(8,128)(2,1)S(1)}, u32[]{:S(2)}, u32[]{:S(2)}) async-start(bf16[16,64,896]{2,1,0:T(8,128)(2,1)} %bitcast.25), calls=%async_computation.2 | async-start | bytes 3670016 | tf_op jit(solution)/shard_map/all_to_all | solution.py:46
  147.8 16.3 %all-to-all-done.2 = bf16[16,64,896]{2,1,0:T(8,128)(2,1)S(1)} async-done(((bf16[16,64,896]{2,1,0:T(8,128)(2,1)}), bf16[16,64,896]{2,1,0:T(8,128)(2,1)S(1)}, u32[]{:S(2)}, u32[]{:S(2)}) %all-to-all-start.2) | async-done | bytes 1835040 | tf_op jit(solution)/shard_map/all_to_all | solution.py:46
  166.4 6.8 %collective-permute-done.13 = bf16[64,896]{1,0:T(8,128)(2,1)S(1)} collective-permute-done((bf16[64,896]{1,0:T(8,128)(2,1)}, bf16[64,896]{1,0:T(8,128)(2,1)S(1)}, u32[]{:S(2)}, u32[]{:S(2)}) %collective-permute-start.13) | collective-permute-done | bytes 114720 | tf_op jit(solution)/shard_map/ppermute | solution.py:27
  174.2 1.5 broadcast_in_dim.14
  175.7 10.5 %all-to-all-start.3 = ((bf16[16,64,896]{2,1,0:T(8,128)(2,1)}), bf16[16,64,896]{2,1,0:T(8,128)(2,1)S(1)}, u32[]{:S(2)}, u32[]{:S(2)}) async-start(bf16[16,64,896]{2,1,0:T(8,128)(2,1)} %broadcast_in_dim.14), calls=%async_computation.3 | async-start | bytes 3670016 | tf_op jit(solution)/shard_map/all_to_all | solution.py:46
  188.2 13.6 %collective-permute-done.14 = bf16[1152,256]{1,0:T(8,128)(2,1)} collective-permute-done((bf16[1152,256]{1,0:T(8,128)(2,1)}, bf16[1152,256]{1,0:T(8,128)(2,1)}, u32[]{:S(2)}, u32[]{:S(2)}) %collective-permute-start.14) | collective-permute-done | bytes 589856 | tf_op jit(solution)/shard_map/ppermute | solution.py:27
  201.8 9.0 %all-to-all-done.3 = bf16[16,64,896]{2,1,0:T(8,128)(2,1)S(1)} async-done(((bf16[16,64,896]{2,1,0:T(8,128)(2,1)}), bf16[16,64,896]{2,1,0:T(8,128)(2,1)S(1)}, u32[]{:S(2)}, u32[]{:S(2)}) %all-to-all-start.3) | async-done | bytes 1835040 | tf_op jit(solution)/shard_map/all_to_all | solution.py:46
  210.8 1.4 fusion.48
  215.9 2.0 multiply_reduce_fusion
  220.7 3.2 %collective-permute-done.16 = bf16[576,256]{1,0:T(8,128)(2,1)S(1)} collective-permute-done((bf16[576,256]{1,0:T(8,128)(2,1)S(1)}, bf16[576,256]{1,0:T(8,128)(2,1)S(1)}, u32[]{:S(2)}, u32[]{:S(2)}) %collective-permute-start.16) | collective-permute-done | bytes 294944 | tf_op jit(solution)/shard_map/ppermute | solution.py:27
  225.6 2.5 collective-permute-done.20
  228.2 2.3 collective-permute-done.19
  230.5 3.2 %collective-permute-start.21 = (bf16[576,128]{1,0:T(8,128)(2,1)S(1)}, bf16[576,128]{1,0:T(8,128)(2,1)S(1)}, u32[]{:S(2)}, u32[]{:S(2)}) collective-permute-start(bf16[576,128]{1,0:T(8,128)(2,1)S(1)} %fusion.29), channel_id=1, source_target_pairs={{0,4},{2,6},{4,0},{6,2},{1,5},{3,7},{5,1},{7,3},{8,12},{10,14},{12... | collective-permute-start | bytes 442376 | tf_op jit(solution)/shard_map/ppermute | solution.py:27
  235.0 5.2 %collective-permute-done.22 = f32[8,128]{1,0:T(8,128)S(1)} collective-permute-done((f32[8,128]{1,0:T(8,128)S(1)}, f32[8,128]{1,0:T(8,128)S(1)}, u32[]{:S(2)}, u32[]{:S(2)}) %collective-permute-start.22) | collective-permute-done | bytes 4128 | tf_op jit(solution)/shard_map/ppermute | solution.py:27
  240.2 2.5 collective-permute-start.23
  244.1 5.4 %collective-permute-done.23 = bf16[576,256]{1,0:T(8,128)(2,1)S(1)} collective-permute-done((bf16[576,256]{1,0:T(8,128)(2,1)S(1)}, bf16[576,256]{1,0:T(8,128)(2,1)S(1)}, u32[]{:S(2)}, u32[]{:S(2)}) %collective-permute-start.23) | collective-permute-done | bytes 294944 | tf_op jit(solution)/shard_map/ppermute | solution.py:27
  (163 shorter events, 39.2 us)
Async XLA Ops:
  0.6 16.1 %copy-start.1 = (bf16[896,576]{0,1:T(8,128)(2,1)S(1)}, bf16[896,576]{0,1:T(8,128)(2,1)}, u32[]{:S(2)}) copy-start(bf16[896,576]{0,1:T(8,128)(2,1)} %param.15) | copy-start | bytes 3096580
  0.6 16.1 %copy-start.2 = (bf16[896,576]{0,1:T(8,128)(2,1)S(1)}, bf16[896,576]{0,1:T(8,128)(2,1)}, u32[]{:S(2)}) copy-start(bf16[896,576]{0,1:T(8,128)(2,1)} %param.16) | copy-start | bytes 3096580
  0.7 16.0 %copy-start.21 = (f32[2,576]{1,0:T(2,128)S(1)}, f32[2,576]{1,0:T(2,128)}, u32[]{:S(2)}) copy-start(f32[2,576]{1,0:T(2,128)} %param.21) | copy-start | bytes 13828
  0.7 16.0 %copy-start.20 = (s32[2,576]{1,0:T(2,128)S(1)}, s32[2,576]{1,0:T(2,128)}, u32[]{:S(2)}) copy-start(s32[2,576]{1,0:T(2,128)} %param.22) | copy-start | bytes 13828
  0.7 15.9 %copy-start.19 = (s32[2,576]{1,0:T(2,128)S(1)}, s32[2,576]{1,0:T(2,128)}, u32[]{:S(2)}) copy-start(s32[2,576]{1,0:T(2,128)} %param.23) | copy-start | bytes 13828
  0.7 15.9 %collective-permute-start = (bf16[32,896]{1,0:T(8,128)(2,1)}, bf16[32,896]{1,0:T(8,128)(2,1)S(1)}, u32[]{:S(2)}, u32[]{:S(2)}) collective-permute-start(bf16[32,896]{1,0:T(8,128)(2,1)} %param.14), channel_id=1, source_target_pairs={{0,8},{8,0},{1,9},{9,1},{2,10},{10,2},{3,11},{11,3},{4,12},{12,4},... | collective-permute-start | bytes 172040 | tf_op jit(solution)/shard_map/ppermute | solution.py:27
  7.7 21.6 %all-to-all-start = ((bf16[16,32,896]{2,1,0:T(8,128)(2,1)}), bf16[16,32,896]{2,1,0:T(8,128)(2,1)S(1)}, u32[]{:S(2)}, u32[]{:S(2)}) async-start(bf16[16,32,896]{2,1,0:T(8,128)(2,1)} %broadcast_in_dim.12), calls=%async_computation | async-start | bytes 1835008 | tf_op jit(solution)/shard_map/all_to_all | solution.py:46
  29.3 3.5 %copy-start.3 = (bf16[16,32,896]{2,1,0:T(8,128)(2,1)}, bf16[16,32,896]{2,1,0:T(8,128)(2,1)S(1)}, u32[]{:S(2)}) copy-start(bf16[16,32,896]{2,1,0:T(8,128)(2,1)S(1)} %all-to-all-done) | copy-start | bytes 2752516
  29.3 3.5 %copy-start.9 = (bf16[1152,896]{1,0:T(8,128)(2,1)S(1)}, bf16[1152,896]{1,0:T(8,128)(2,1)}, u32[]{:S(2)}) copy-start(bf16[1152,896]{1,0:T(8,128)(2,1)} %pad_maximum_fusion) | copy-start | bytes 6193156
  32.8 3.8 %copy-start.14 = (f32[512,1152]{1,0:T(8,128)}, f32[512,1152]{1,0:T(8,128)S(1)}, u32[]{:S(2)}) copy-start(f32[512,1152]{1,0:T(8,128)S(1)} %convolution_bitcast_fusion) | copy-start | bytes 7077892
  36.2 9.6 %collective-permute-start.1 = (bf16[2,256,1152]{2,1,0:T(8,128)(2,1)}, bf16[2,256,1152]{2,1,0:T(8,128)(2,1)}, u32[]{:S(2)}, u32[]{:S(2)}) collective-permute-start(bf16[2,256,1152]{2,1,0:T(8,128)(2,1)} %pad_maximum_fusion.4), channel_id=1, source_target_pairs={{0,1},{1,0},{2,3},{3,2},{4,5},{5,4},{6,7},{7,6},{8,9},{9,8},{10,11... | collective-permute-start | bytes 3538952 | tf_op jit(solution)/shard_map/ppermute | solution.py:27
  37.6 8.2 %copy-start.13 = (f32[512,1152]{1,0:T(8,128)S(1)}, f32[512,1152]{1,0:T(8,128)}, u32[]{:S(2)}) copy-start(f32[512,1152]{1,0:T(8,128)} %copy-done.12) | copy-start | bytes 7077892
  37.6 17.5 %all-to-all-start.1 = ((bf16[16,32,896]{2,1,0:T(8,128)(2,1)}), bf16[16,32,896]{2,1,0:T(8,128)(2,1)S(1)}, u32[]{:S(2)}, u32[]{:S(2)}) async-start(bf16[16,32,896]{2,1,0:T(8,128)(2,1)} %broadcast_in_dim.13), calls=%async_computation.1 | async-start | bytes 1835008 | tf_op jit(solution)/shard_map/all_to_all | solution.py:46
  48.3 14.8 %collective-permute-start.2 = (bf16[2,128,1152]{2,1,0:T(8,128)(2,1)}, bf16[2,128,1152]{2,1,0:T(8,128)(2,1)}, u32[]{:S(2)}, u32[]{:S(2)}) collective-permute-start(bf16[2,128,1152]{2,1,0:T(8,128)(2,1)} %slice.322), channel_id=1, source_target_pairs={{0,2},{2,0},{4,6},{6,4},{1,3},{3,1},{5,7},{7,5},{8,10},{10,8},{12,... | collective-permute-start | bytes 1769480 | tf_op jit(solution)/shard_map/ppermute | solution.py:27
  55.2 3.5 %copy-start.5 = (bf16[16,32,896]{2,1,0:T(8,128)(2,1)}, bf16[16,32,896]{2,1,0:T(8,128)(2,1)S(1)}, u32[]{:S(2)}) copy-start(bf16[16,32,896]{2,1,0:T(8,128)(2,1)S(1)} %all-to-all-done.1) | copy-start | bytes 2752516
  55.2 3.5 %copy-start.10 = (bf16[1152,896]{1,0:T(8,128)(2,1)S(1)}, bf16[1152,896]{1,0:T(8,128)(2,1)}, u32[]{:S(2)}) copy-start(bf16[1152,896]{1,0:T(8,128)(2,1)} %pad_maximum_fusion) | copy-start | bytes 6193156
  60.5 5.1 %collective-permute-start.6 = (bf16[2,256,1152]{2,1,0:T(8,128)(2,1)S(1)}, bf16[2,256,1152]{2,1,0:T(8,128)(2,1)S(1)}, u32[]{:S(2)}, u32[]{:S(2)}) collective-permute-start(bf16[2,256,1152]{2,1,0:T(8,128)(2,1)S(1)} %pad_maximum_fusion.5), channel_id=1, source_target_pairs={{0,1},{1,0},{2,3},{3,2},{4,5},{5,4},{6,7},{7,6},{8,9},{9,8},{10,11... | collective-permute-start | bytes 3538952 | tf_op jit(solution)/shard_map/ppermute | solution.py:27
  64.4 14.0 %collective-permute-start.3 = (bf16[2,64,1152]{2,1,0:T(8,128)(2,1)S(1)}, bf16[2,64,1152]{2,1,0:T(8,128)(2,1)S(1)}, u32[]{:S(2)}, u32[]{:S(2)}) collective-permute-start(bf16[2,64,1152]{2,1,0:T(8,128)(2,1)S(1)} %slice.324), channel_id=1, source_target_pairs={{0,4},{2,6},{4,0},{6,2},{1,5},{3,7},{5,1},{7,3},{8,12},{10,14},{12... | collective-permute-start | bytes 884744 | tf_op jit(solution)/shard_map/ppermute | solution.py:27
  65.9 19.9 %collective-permute-start.7 = (bf16[2,128,1152]{2,1,0:T(8,128)(2,1)S(1)}, bf16[2,128,1152]{2,1,0:T(8,128)(2,1)S(1)}, u32[]{:S(2)}, u32[]{:S(2)}) collective-permute-start(bf16[2,128,1152]{2,1,0:T(8,128)(2,1)S(1)} %slice.321), channel_id=1, source_target_pairs={{0,2},{2,0},{4,6},{6,4},{1,3},{3,1},{5,7},{7,5},{8,10},{10,8},{12,... | collective-permute-start | bytes 1769480 | tf_op jit(solution)/shard_map/ppermute | solution.py:27
  85.9 30.5 %copy-start.23 = (f32[896]{0:T(1024)S(1)}, f32[896]{0:T(1024)}, u32[]{:S(2)}) copy-start(f32[896]{0:T(1024)} %param.24) | copy-start | bytes 10756
  85.9 30.5 %copy-start.24 = (s32[896]{0:T(1024)S(1)}, s32[896]{0:T(1024)}, u32[]{:S(2)}) copy-start(s32[896]{0:T(1024)} %param.26) | copy-start | bytes 10756
  85.9 18.4 %collective-permute-start.8 = (bf16[2,64,1152]{2,1,0:T(8,128)(2,1)S(1)}, bf16[2,64,1152]{2,1,0:T(8,128)(2,1)S(1)}, u32[]{:S(2)}, u32[]{:S(2)}) collective-permute-start(bf16[2,64,1152]{2,1,0:T(8,128)(2,1)S(1)} %slice.323), channel_id=1, source_target_pairs={{0,4},{2,6},{4,0},{6,2},{1,5},{3,7},{5,1},{7,3},{8,12},{10,14},{12... | collective-permute-start | bytes 884744 | tf_op jit(solution)/shard_map/ppermute | solution.py:27
  88.3 19.4 %collective-permute-start.4 = (bf16[64,1152]{1,0:T(8,128)(2,1)S(1)}, bf16[64,1152]{1,0:T(8,128)(2,1)S(1)}, u32[]{:S(2)}, u32[]{:S(2)}) collective-permute-start(bf16[64,1152]{1,0:T(8,128)(2,1)S(1)} %fusion.34), channel_id=1, source_target_pairs={{0,4},{2,6},{4,0},{6,2},{1,5},{3,7},{5,1},{7,3},{8,12},{10,14},{12... | collective-permute-start | bytes 442376 | tf_op jit(solution)/shard_map/ppermute | solution.py:27
  104.5 9.3 %collective-permute-start.9 = (bf16[64,1152]{1,0:T(8,128)(2,1)S(1)}, bf16[64,1152]{1,0:T(8,128)(2,1)S(1)}, u32[]{:S(2)}, u32[]{:S(2)}) collective-permute-start(bf16[64,1152]{1,0:T(8,128)(2,1)S(1)} %fusion.30), channel_id=1, source_target_pairs={{0,4},{2,6},{4,0},{6,2},{1,5},{3,7},{5,1},{7,3},{8,12},{10,14},{12... | collective-permute-start | bytes 442376 | tf_op jit(solution)/shard_map/ppermute | solution.py:27
  107.7 11.4 %collective-permute-start.5 = (bf16[128,1152]{1,0:T(8,128)(2,1)S(1)}, bf16[128,1152]{1,0:T(8,128)(2,1)S(1)}, u32[]{:S(2)}, u32[]{:S(2)}) collective-permute-start(bf16[128,1152]{1,0:T(8,128)(2,1)S(1)} %pad_maximum_fusion.14), channel_id=1, source_target_pairs={{0,2},{2,0},{4,6},{6,4},{1,3},{3,1},{5,7},{7,5},{8,10},{10,8},{12,... | collective-permute-start | bytes 884744 | tf_op jit(solution)/shard_map/ppermute | solution.py:27
  113.8 11.6 %collective-permute-start.10 = (bf16[128,1152]{1,0:T(8,128)(2,1)S(1)}, bf16[128,1152]{1,0:T(8,128)(2,1)S(1)}, u32[]{:S(2)}, u32[]{:S(2)}) collective-permute-start(bf16[128,1152]{1,0:T(8,128)(2,1)S(1)} %pad_maximum_fusion.15), channel_id=1, source_target_pairs={{0,2},{2,0},{4,6},{6,4},{1,3},{3,1},{5,7},{7,5},{8,10},{10,8},{12,... | collective-permute-start | bytes 884744 | tf_op jit(solution)/shard_map/ppermute | solution.py:27
  119.2 7.7 %copy-start = (bf16[576,896]{1,0:T(8,128)(2,1)S(1)}, bf16[576,896]{1,0:T(8,128)(2,1)}, u32[]{:S(2)}) copy-start(bf16[576,896]{1,0:T(8,128)(2,1)} %param.17) | copy-start | bytes 3096580
  119.2 7.7 %copy-start.15 = (bf16[576,896]{1,0:T(8,128)(2,1)S(1)}, bf16[576,896]{1,0:T(8,128)(2,1)}, u32[]{:S(2)}) copy-start(bf16[576,896]{1,0:T(8,128)(2,1)} %param.20) | copy-start | bytes 3096580
  125.6 3.7 %copy-start.7 = (bf16[8,2,32,1152]{3,2,1,0:T(8,128)(2,1)}, bf16[8,2,32,1152]{3,2,1,0:T(8,128)(2,1)S(1)}, u32[]{:S(2)}) copy-start(bf16[8,2,32,1152]{3,2,1,0:T(8,128)(2,1)S(1)} %pad_maximum_fusion.6) | copy-start | bytes 3538948
  125.6 5.1 %collective-permute-start.11 = (bf16[512,1152]{1,0:T(8,128)(2,1)S(1)}, bf16[512,1152]{1,0:T(8,128)(2,1)S(1)}, u32[]{:S(2)}, u32[]{:S(2)}) collective-permute-start(bf16[512,1152]{1,0:T(8,128)(2,1)S(1)} %bitcast.134), channel_id=1, source_target_pairs={{0,1},{1,0},{2,3},{3,2},{4,5},{5,4},{6,7},{7,6},{8,9},{9,8},{10,11... | collective-permute-start | bytes 3538952 | tf_op jit(solution)/shard_map/ppermute | solution.py:27
  133.7 30.5 %all-to-all-start.2 = ((bf16[16,64,896]{2,1,0:T(8,128)(2,1)}), bf16[16,64,896]{2,1,0:T(8,128)(2,1)S(1)}, u32[]{:S(2)}, u32[]{:S(2)}) async-start(bf16[16,64,896]{2,1,0:T(8,128)(2,1)} %bitcast.25), calls=%async_computation.2 | async-start | bytes 3670016 | tf_op jit(solution)/shard_map/all_to_all | solution.py:46
  143.7 4.1 %copy-start.18 = (f32[1024]{0:T(1024)S(1)}, f32[1024]{0:T(1024)}, u32[]{:S(2)}) copy-start(f32[1024]{0:T(1024)} %param.27) | copy-start | bytes 12292
  147.0 18.1 %collective-permute-start.12 = (bf16[1152,128]{1,0:T(8,128)(2,1)S(1)}, bf16[1152,128]{1,0:T(8,128)(2,1)S(1)}, u32[]{:S(2)}, u32[]{:S(2)}) collective-permute-start(bf16[1152,128]{1,0:T(8,128)(2,1)S(1)} %pad_maximum_fusion.16), channel_id=1, source_target_pairs={{0,4},{2,6},{4,0},{6,2},{1,5},{3,7},{5,1},{7,3},{8,12},{10,14},{12... | collective-permute-start | bytes 884744 | tf_op jit(solution)/shard_map/ppermute | solution.py:27
  165.1 8.1 %collective-permute-start.13 = (bf16[64,896]{1,0:T(8,128)(2,1)}, bf16[64,896]{1,0:T(8,128)(2,1)S(1)}, u32[]{:S(2)}, u32[]{:S(2)}) collective-permute-start(bf16[64,896]{1,0:T(8,128)(2,1)} %reduce_sum.21), channel_id=1, source_target_pairs={{0,8},{8,0},{1,9},{9,1},{2,10},{10,2},{3,11},{11,3},{4,12},{12,4},... | collective-permute-start | bytes 344072 | tf_op jit(solution)/shard_map/ppermute | solution.py:27
  175.7 35.1 %all-to-all-start.3 = ((bf16[16,64,896]{2,1,0:T(8,128)(2,1)}), bf16[16,64,896]{2,1,0:T(8,128)(2,1)S(1)}, u32[]{:S(2)}, u32[]{:S(2)}) async-start(bf16[16,64,896]{2,1,0:T(8,128)(2,1)} %broadcast_in_dim.14), calls=%async_computation.3 | async-start | bytes 3670016 | tf_op jit(solution)/shard_map/all_to_all | solution.py:46
  187.2 14.6 %collective-permute-start.14 = (bf16[1152,256]{1,0:T(8,128)(2,1)}, bf16[1152,256]{1,0:T(8,128)(2,1)}, u32[]{:S(2)}, u32[]{:S(2)}) collective-permute-start(bf16[1152,256]{1,0:T(8,128)(2,1)} %pad_maximum_fusion.12), channel_id=1, source_target_pairs={{0,2},{2,0},{4,6},{6,4},{1,3},{3,1},{5,7},{7,5},{8,10},{10,8},{12,... | collective-permute-start | bytes 1769480 | tf_op jit(solution)/shard_map/ppermute | solution.py:27
  212.3 3.4 %collective-permute-start.15 = (bf16[576,512]{1,0:T(8,128)(2,1)S(1)}, bf16[576,512]{1,0:T(8,128)(2,1)S(1)}, u32[]{:S(2)}, u32[]{:S(2)}) collective-permute-start(bf16[576,512]{1,0:T(8,128)(2,1)S(1)} %slice.320), channel_id=1, source_target_pairs={{0,1},{1,0},{2,3},{3,2},{4,5},{5,4},{6,7},{7,6},{8,9},{9,8},{10,11... | collective-permute-start | bytes 1769480 | tf_op jit(solution)/shard_map/ppermute | solution.py:27
  214.5 9.4 %collective-permute-start.18 = (bf16[1152,512]{1,0:T(8,128)(2,1)S(1)}, bf16[1152,512]{1,0:T(8,128)(2,1)S(1)}, u32[]{:S(2)}, u32[]{:S(2)}) collective-permute-start(bf16[1152,512]{1,0:T(8,128)(2,1)S(1)} %constant_dynamic-update-slice_fusion), channel_id=1, source_target_pairs={{0,1},{1,0},{2,3},{3,2},{4,5},{5,4},{6,7},{7,6},{8,9},{9,8},{10,11... | collective-permute-start | bytes 3538952 | tf_op jit(solution)/shard_map/ppermute | solution.py:27
  215.8 8.2 %collective-permute-start.16 = (bf16[576,256]{1,0:T(8,128)(2,1)S(1)}, bf16[576,256]{1,0:T(8,128)(2,1)S(1)}, u32[]{:S(2)}, u32[]{:S(2)}) collective-permute-start(bf16[576,256]{1,0:T(8,128)(2,1)S(1)} %fusion.27), channel_id=1, source_target_pairs={{0,2},{2,0},{4,6},{6,4},{1,3},{3,1},{5,7},{7,5},{8,10},{10,8},{12,... | collective-permute-start | bytes 884744 | tf_op jit(solution)/shard_map/ppermute | solution.py:27
  218.5 1.6 collective-permute-start.17
  224.1 6.4 %collective-permute-start.19 = (bf16[576,128]{1,0:T(8,128)(2,1)S(1)}, bf16[576,128]{1,0:T(8,128)(2,1)S(1)}, u32[]{:S(2)}, u32[]{:S(2)}) collective-permute-start(bf16[576,128]{1,0:T(8,128)(2,1)S(1)} %slice.325), channel_id=1, source_target_pairs={{0,4},{2,6},{4,0},{6,2},{1,5},{3,7},{5,1},{7,3},{8,12},{10,14},{12... | collective-permute-start | bytes 442376 | tf_op jit(solution)/shard_map/ppermute | solution.py:27
  224.5 3.7 %collective-permute-start.20 = (f32[8,128]{1,0:T(8,128)S(1)}, f32[8,128]{1,0:T(8,128)S(1)}, u32[]{:S(2)}, u32[]{:S(2)}) collective-permute-start(f32[8,128]{1,0:T(8,128)S(1)} %broadcast_add_fusion), channel_id=1, source_target_pairs={{0,2},{2,0},{4,6},{6,4},{1,3},{3,1},{5,7},{7,5},{8,10},{10,8},{12,... | collective-permute-start | bytes 12296 | tf_op jit(solution)/shard_map/ppermute | solution.py:27
  230.5 12.2 %copy-start.4 = (bf16[16,32,896]{2,1,0:T(8,128)(2,1)S(1)}, bf16[16,32,896]{2,1,0:T(8,128)(2,1)}, u32[]{:S(2)}) copy-start(bf16[16,32,896]{2,1,0:T(8,128)(2,1)} %copy-done.3) | copy-start | bytes 2752516
  230.5 12.2 %copy-start.6 = (bf16[16,32,896]{2,1,0:T(8,128)(2,1)S(1)}, bf16[16,32,896]{2,1,0:T(8,128)(2,1)}, u32[]{:S(2)}) copy-start(bf16[16,32,896]{2,1,0:T(8,128)(2,1)} %copy-done.5) | copy-start | bytes 2752516
  230.5 9.6 %collective-permute-start.21 = (bf16[576,128]{1,0:T(8,128)(2,1)S(1)}, bf16[576,128]{1,0:T(8,128)(2,1)S(1)}, u32[]{:S(2)}, u32[]{:S(2)}) collective-permute-start(bf16[576,128]{1,0:T(8,128)(2,1)S(1)} %fusion.29), channel_id=1, source_target_pairs={{0,4},{2,6},{4,0},{6,2},{1,5},{3,7},{5,1},{7,3},{8,12},{10,14},{12... | collective-permute-start | bytes 442376 | tf_op jit(solution)/shard_map/ppermute | solution.py:27
  233.7 6.4 %collective-permute-start.22 = (f32[8,128]{1,0:T(8,128)S(1)}, f32[8,128]{1,0:T(8,128)S(1)}, u32[]{:S(2)}, u32[]{:S(2)}) collective-permute-start(f32[8,128]{1,0:T(8,128)S(1)} %add.158), channel_id=1, source_target_pairs={{0,4},{2,6},{4,0},{6,2},{1,5},{3,7},{5,1},{7,3},{8,12},{10,14},{12... | collective-permute-start | bytes 12296 | tf_op jit(solution)/shard_map/ppermute | solution.py:27
  240.2 9.4 %collective-permute-start.23 = (bf16[576,256]{1,0:T(8,128)(2,1)S(1)}, bf16[576,256]{1,0:T(8,128)(2,1)S(1)}, u32[]{:S(2)}, u32[]{:S(2)}) collective-permute-start(bf16[576,256]{1,0:T(8,128)(2,1)S(1)} %pad_maximum_fusion.17), channel_id=1, source_target_pairs={{0,2},{2,0},{4,6},{6,4},{1,3},{3,1},{5,7},{7,5},{8,10},{10,8},{12,... | collective-permute-start | bytes 884744 | tf_op jit(solution)/shard_map/ppermute | solution.py:27
  249.6 2.8 %collective-permute-start.24 = (bf16[576,512]{1,0:T(8,128)(2,1)S(1)}, bf16[576,512]{1,0:T(8,128)(2,1)S(1)}, u32[]{:S(2)}, u32[]{:S(2)}) collective-permute-start(bf16[576,512]{1,0:T(8,128)(2,1)S(1)} %pad_maximum_fusion.13), channel_id=1, source_target_pairs={{0,1},{1,0},{2,3},{3,2},{4,5},{5,4},{6,7},{7,6},{8,9},{9,8},{10,11... | collective-permute-start | bytes 1769480 | tf_op jit(solution)/shard_map/ppermute | solution.py:27
  (6 other events, 14.1 us)
